TPU v7x, 256 devices: a whole 4x4x8 slice. The times are simulated.
256 devices in a mesh: row: 8 (over z), col: 32 (over x, y, core).
Axes of the slice: x: 4, y: 4, z: 8, core: 2. Of those that a mesh axis runs over, the one named last changes fastest.
Arguments:
- rhs: float32 [64, 131072], P(None, ('row', 'col')), may hold values from -6 to 6
- pivots: int32 [4096], replicated, may hold values from 0 to 131071, as said below
- factor: float32 [4096, 1, 32, 128], P('row', None, 'col'), as said below
- diag_inv: float32 [8, 512, 512], P('row'), as said below
Outputs:
- solution: float32 [64, 1, 32, 128], P(None, None, 'col')
Inputs may be any that keep to these rules, and one draw needn't show every extreme that they name: `pivots`: distinct column numbers, the first 4096 entries of a permutation of 0 .. 131071. `factor`: entry (row i, column q) is zero where q >= 512 * (i // 512). `diag_inv`: each block is unit lower triangular.
All inputs are finite; a program needn't handle non-finite values.
Results may differ from a plain program's by a relative error of at most 0.0001.
Values sent between devices are 32-bit elements; how exact they have to be, the bound alone decides.
No kernel may reach another device: no remote copies, remote signals or barrier semaphores. Data moves between devices by JAX's collectives and lax.ppermute only.
A program may use at most 64 MiB of HBM per device.

v0:
```python
import functools

import jax
import jax.numpy as jnp
from jax import lax
from jax.experimental import pallas as pl
from jax.experimental.pallas import tpu as pltpu
from jax.sharding import Mesh
from jax.sharding import PartitionSpec as P


QUAD = 4
VMEM_LIMIT = 16 * 2**20


def dot(a, b, contract):
    return lax.dot_general(
        a,
        b,
        (contract, ((), ())),
        precision=lax.Precision.HIGHEST,
        preferred_element_type=jnp.float32,
    )


def split3(x):
    hi = x.astype(jnp.bfloat16)
    rest = x - hi.astype(jnp.float32)
    mid = rest.astype(jnp.bfloat16)
    lo = (rest - mid.astype(jnp.float32)).astype(jnp.bfloat16)
    return hi, mid, lo


def take_kernel(first_ref, pivots_ref, rhs_ref, out_ref):
    count, source = rhs_ref.shape
    located = pivots_ref[...] - first_ref[0]
    place = lax.broadcasted_iota(jnp.int32, (source, located.shape[1]), 0)
    pick = jnp.where(place == located, 1.0, 0.0).astype(jnp.bfloat16)
    parts = jnp.concatenate(split3(rhs_ref[...]), axis=0)
    got = jnp.dot(parts, pick, preferred_element_type=jnp.float32)
    got = (got[2 * count :] + got[count : 2 * count]) + got[:count]
    pieces, _, length = out_ref.shape
    for n in range(pieces):
        out_ref[n] = got[:, n * length : (n + 1) * length]


def take_columns(rhs, pivots, first, piece_len):
    count, source = rhs.shape
    total = pivots.shape[0]
    step = source
    return pl.pallas_call(
        take_kernel,
        grid=(total // step,),
        in_specs=[
            pl.BlockSpec(memory_space=pltpu.SMEM),
            pl.BlockSpec((1, step), lambda n: (0, n)),
            pl.BlockSpec((count, source), lambda n: (0, 0)),
        ],
        out_specs=pl.BlockSpec((step // piece_len, count, piece_len), lambda n: (n, 0, 0)),
        out_shape=jax.ShapeDtypeStruct((total // piece_len, count, piece_len), jnp.float32),
        compiler_params=pltpu.CompilerParams(vmem_limit_bytes=VMEM_LIMIT),
    )(first.reshape(1), pivots.reshape(1, total), rhs)


def split2(x):
    hi = x.astype(jnp.bfloat16)
    return hi, (x - hi.astype(jnp.float32)).astype(jnp.bfloat16)


NN = ((1,), (0,))
NT = ((1,), (1,))


def product(y, hi, mid, contract):
    rows = y.shape[0]
    y_hi, y_mid = split2(y)

    def mul(a, b):
        return lax.dot_general(a, b, (contract, ((), ())), preferred_element_type=jnp.float32)

    wide = mul(jnp.concatenate([y_hi, y_mid], axis=0), hi)
    return wide[:rows] + (wide[rows:] + mul(y_hi, mid))


def prep_kernel(parts, flags_ref, *refs):
    count = len(parts)
    mine, theirs = refs[:count], refs[count : 2 * count]
    hi_ref, mid_ref = refs[-2:]
    rows = hi_ref.shape[0]
    length = mine[0].shape[0]
    core = flags_ref[0]

    def put(row, place, offset, value):
        start = pl.multiple_of(place * length + offset, value.shape[0])
        at = pl.ds(start, value.shape[0])
        hi_ref[row, at, :], mid_ref[row, at, :] = split2(value)

    for n, (distance, offset) in enumerate(parts):
        row = lax.rem(flags_ref[3] + (distance + rows), rows)
        put(row, core, offset, mine[n][...])
        put(row, 1 - core, offset, theirs[n][...])


def prepare(flags, rows, parts, mine, theirs):
    length, width = mine[0].shape
    shape = (rows, 2 * length, width)
    vmem = pl.BlockSpec(memory_space=pltpu.VMEM)
    return pl.pallas_call(
        functools.partial(prep_kernel, parts),
        in_specs=[pl.BlockSpec(memory_space=pltpu.SMEM)] + [vmem] * (len(mine) + len(theirs)),
        out_specs=[vmem, vmem],
        out_shape=[pltpu.VMEM(shape, jnp.bfloat16)] * 2,
        compiler_params=pltpu.CompilerParams(vmem_limit_bytes=VMEM_LIMIT),
    )(flags, *mine, *theirs)


def contributions(step, flags_ref, y, earlier, hi_ref, mid_ref, same_ref, sent_ref):
    half_len = y.shape[1]
    for n in range(step + 1, hi_ref.shape[0]):
        got = product(y, hi_ref[n], mid_ref[n], NN)
        low, high = got[:, :half_len], got[:, half_len:]
        k = n - step - 1
        if earlier is not None:
            low = low + earlier[1 + 2 * k]
            high = high + earlier[2 + 2 * k]
        if k == 0:
            same_ref[...] = jnp.where(flags_ref[1] == 0, low, high)
            sent_ref[0] = jnp.where(flags_ref[1] == 0, high, low)
        else:
            sent_ref[2 * k - 1] = low
            sent_ref[2 * k] = high


def first_kernel(flags_ref, pieces_ref, hi_ref, mid_ref, start_ref, same_ref, sent_ref):
    sums = jnp.sum(pieces_ref[...], axis=0)
    block = jnp.concatenate([sums[i] for i in range(QUAD)], axis=1)
    own = flags_ref[2]
    start = product(block, hi_ref[own], mid_ref[own], NT)
    start_ref[...] = start
    contributions(0, flags_ref, start, None, hi_ref, mid_ref, same_ref, sent_ref)


def step_kernel(step, flags_ref, start_ref, near_ref, far_ref, final_ref, *rest):
    both = start_ref[...] + near_ref[0] + far_ref[...]
    kept = jnp.where(flags_ref[2] == step, both, final_ref[...])
    if len(rest) == 1:
        rest[0][...] = kept
        return
    hi_ref, mid_ref, kept_ref, same_ref, sent_ref = rest
    kept_ref[...] = kept
    contributions(step, flags_ref, both, near_ref, hi_ref, mid_ref, same_ref, sent_ref)


def call(kernel, flags, args, outs):
    vmem = pl.BlockSpec(memory_space=pltpu.VMEM)
    return pl.pallas_call(
        kernel,
        in_specs=[pl.BlockSpec(memory_space=pltpu.SMEM)] + [vmem] * len(args),
        out_specs=[vmem] * len(outs),
        out_shape=[jax.ShapeDtypeStruct(shape, jnp.float32) for shape in outs],
        compiler_params=pltpu.CompilerParams(vmem_limit_bytes=VMEM_LIMIT),
    )(flags, *args)


def next_quad(quad, step, quads):
    if step % 2 == 0:
        return quad ^ 1
    return (quad + (1 if quad % 2 else -1)) % quads


def solve(rhs, pivots, factor, diag_inv):
    my_row = lax.axis_index("row")
    my_quad = lax.axis_index("quad")
    my_i = lax.axis_index("i")
    rows = lax.axis_size("row")
    quads = lax.axis_size("quad")
    core = my_i % 2
    half = my_i // 2
    rhs_count, source_len = rhs.shape
    block_len, _, _, piece_len = factor.shape
    group = rhs_count // rows
    flat = (my_row * quads + my_quad) * QUAD + my_i
    places = [(q, i) for q in range(quads) for i in range(QUAD)]

    def pairs(move):
        return [(q * QUAD + i, move(q, i)[0] * QUAD + move(q, i)[1]) for q, i in places]

    lower = factor.reshape(block_len, piece_len)
    inverse = diag_inv[0]
    scaled = dot(lower, inverse, ((0,), (1,)))
    own_rows = lax.dynamic_slice_in_dim(inverse, my_i * piece_len, piece_len, 0)
    slot = jnp.where(my_quad == my_row, own_rows, -scaled)

    def shift(shard, by):
        return lax.ppermute(shard, "row", [(r, (r + by) % rows) for r in range(rows)])

    partner = [(i, i ^ 1) for i in range(QUAD)]
    first = [shift(slot, 2), shift(slot, -2)]
    first += [shift(slot, 1), shift(slot, -1)]
    taken = take_columns(rhs, pivots, flat * source_len, piece_len)
    spread = lax.all_to_all(taken, ("quad", "i"), 0, 0, tiled=True)
    piece = spread.sum(axis=0)
    cut = piece_len // 2
    second = [
        shift(first[0][:cut], 2),
        shift(first[1][cut:], -2),
        shift(first[0], 1),
        shift(first[1], -1),
    ]
    parts = ((0, 0), (-2, 0), (2, 0), (-1, 0), (1, 0), (4, 0), (4, cut), (-3, 0), (3, 0))
    near_rows = [slot, *first]
    theirs = [lax.ppermute(rows_of, "i", partner) for rows_of in near_rows]
    outgoing = jnp.broadcast_to(
        piece.reshape(rows, 1, group, piece_len), (rows, QUAD, group, piece_len)
    ).reshape(rows * QUAD, group, piece_len)
    incoming = lax.all_to_all(outgoing, ("row", "i"), 0, 0, tiled=True)
    incoming, *second = lax.optimization_barrier((incoming, *second))
    theirs += [lax.ppermute(rows_of, "i", partner) for rows_of in second]
    flags = jnp.stack([core, half, my_quad, my_row]).astype(jnp.int32)
    hi, mid = prepare(flags, rows, parts, near_rows + second, theirs)
    wide = (group, 2 * piece_len)

    def sent_shape(step):
        return (2 * (quads - 2 - step) + 1, *wide)

    start, same, sent = call(
        first_kernel,
        flags,
        (incoming.reshape(rows, QUAD, group, piece_len), hi, mid),
        (wide, wide, sent_shape(0)),
    )
    final = start
    for step in range(quads - 1):
        far_to = pairs(lambda q, i: (next_quad(q, step, quads), i))
        near_to = pairs(lambda q, i: (next_quad(q, step, quads), i ^ 2))
        far = lax.ppermute(same, ("quad", "i"), far_to)
        got = lax.ppermute(sent, ("quad", "i"), near_to)
        args, outs = (start, got, far, final), (wide,)
        if step + 2 < quads:
            args, outs = (*args, hi, mid), (wide, wide, sent_shape(step + 1))
        final, *rest = call(functools.partial(step_kernel, step + 1), flags, args, outs)
        if rest:
            same, sent = rest
    final = jnp.where(core == 0, final[:, :piece_len], final[:, piece_len:])
    whole = lax.all_to_all(
        jnp.broadcast_to(final[None], (rows, group, piece_len)), "row", 0, 0, tiled=True
    )
    return whole.reshape(rhs_count, 1, 1, piece_len)


def solution(mesh):
    rows, cols = mesh.devices.shape
    grid = Mesh(mesh.devices.reshape(rows, cols // QUAD, QUAD), ("row", "quad", "i"))
    return jax.shard_map(
        solve,
        mesh=grid,
        in_specs=(
            P(None, ("row", "quad", "i")),
            P(),
            P("row", None, ("quad", "i"), None),
            P("row", None, None),
        ),
        out_specs=P(None, None, ("quad", "i"), None),
        check_vma=False,
    )
```

profile of v0, /device:TPU:2, one launch (start us, length us, event | category | flops | bytes accessed | tf_op | source)
XLA Modules:
  0.0 145.1 jit_solution(12659036260644559633)
XLA Ops:
  1.7 4.0 %shard_map.46 = f32[32,64,128]{2,1,0:T(8,128)} custom-call(s32[1]{0:T(128)} %bitcast.4.first_ref, s32[1,4096]{1,0:T(1,128)S(1)} %bitcast.19, f32[64,512]{1,0:T(8,128)S(1)} %copy-done.1), custom_call_target="tpu_custom_call" | custom-call | tf_op jit(solution)/shard_map/pallas_call | solution.py:51
  5.7 7.7 %all-to-all-start = ((f32[32,64,128]{2,1,0:T(8,128)}), f32[32,64,128]{2,1,0:T(8,128)}, u32[]{:S(2)}, u32[]{:S(2)}) async-start(f32[32,64,128]{2,1,0:T(8,128)} %shard_map.46), calls=%async_computation | async-start | bytes 2097152 | tf_op jit(solution)/shard_map/all_to_all | solution.py:201
  14.7 6.4 %collective-permute-start.2 = (f32[128,512]{1,0:T(8,128)S(1)}, f32[128,512]{1,0:T(8,128)S(1)}, u32[]{:S(2)}, u32[]{:S(2)}) collective-permute-start(f32[128,512]{1,0:T(8,128)S(1)} %fusion.refs_0_), channel_id=1, source_target_pairs={{0,192},{32,224},{64,0},{96,32},{128,64},{160,96},{192,128},{224,1... | collective-permute-start | bytes 786440 | tf_op jit(solution)/shard_map/ppermute | solution.py:195
  21.0 3.7 %collective-permute-start.7 = (f32[128,512]{1,0:T(8,128)S(1)}, f32[128,512]{1,0:T(8,128)S(1)}, u32[]{:S(2)}, u32[]{:S(2)}) collective-permute-start(f32[128,512]{1,0:T(8,128)S(1)} %fusion.refs_0_), channel_id=1, source_target_pairs={{0,224},{32,0},{64,32},{96,64},{128,96},{160,128},{192,160},{224,1... | collective-permute-start | bytes 786440 | tf_op jit(solution)/shard_map/ppermute | solution.py:195
  24.7 8.2 %collective-permute-done.2.refs_2_ = f32[128,512]{1,0:T(8,128)S(1)} collective-permute-done((f32[128,512]{1,0:T(8,128)S(1)}, f32[128,512]{1,0:T(8,128)S(1)}, u32[]{:S(2)}, u32[]{:S(2)}) %collective-permute-start.2) | collective-permute-done | bytes 262176 | tf_op jit(solution)/shard_map/ppermute | solution.py:195
  32.9 2.7 %collective-permute-start.5 = (f32[128,512]{1,0:T(8,128)S(1)}, f32[128,512]{1,0:T(8,128)S(1)}, u32[]{:S(2)}, u32[]{:S(2)}) collective-permute-start(f32[128,512]{1,0:T(8,128)S(1)} %collective-permute-done.2.refs_2_), channel_id=1, source_target_pairs={{0,224},{32,0},{64,32},{96,64},{128,96},{160,128},{192,160},{224,1... | collective-permute-start | bytes 786440 | tf_op jit(solution)/shard_map/ppermute | solution.py:195
  35.6 2.1 %collective-permute-start.3 = (f32[64,512]{1,0:T(8,128)S(1)}, f32[64,512]{1,0:T(8,128)}, u32[]{:S(2)}, u32[]{:S(2)}) collective-permute-start(f32[64,512]{1,0:T(8,128)S(1)} %slice.17), channel_id=1, source_target_pairs={{0,192},{32,224},{64,0},{96,32},{128,64},{160,96},{192,128},{224,1... | collective-permute-start | bytes 393224 | tf_op jit(solution)/shard_map/ppermute | solution.py:195
  37.8 2.1 %collective-permute-start.4 = (f32[128,512]{1,0:T(8,128)S(1)}, f32[128,512]{1,0:T(8,128)S(1)}, u32[]{:S(2)}, u32[]{:S(2)}) collective-permute-start(f32[128,512]{1,0:T(8,128)S(1)} %collective-permute-done.refs_1_), channel_id=1, source_target_pairs={{0,32},{32,64},{64,96},{96,128},{128,160},{160,192},{192,224},{224... | collective-permute-start | bytes 786440 | tf_op jit(solution)/shard_map/ppermute | solution.py:195
  39.9 2.7 %collective-permute-done.6.refs_3_ = f32[128,512]{1,0:T(8,128)S(1)} collective-permute-done((f32[128,512]{1,0:T(8,128)S(1)}, f32[128,512]{1,0:T(8,128)S(1)}, u32[]{:S(2)}, u32[]{:S(2)}) %collective-permute-start.6) | collective-permute-done | bytes 262176 | tf_op jit(solution)/shard_map/ppermute | solution.py:195
  42.5 6.9 %collective-permute-done.3.refs_6_ = f32[64,512]{1,0:T(8,128)} collective-permute-done((f32[64,512]{1,0:T(8,128)S(1)}, f32[64,512]{1,0:T(8,128)}, u32[]{:S(2)}, u32[]{:S(2)}) %collective-permute-start.3) | collective-permute-done | bytes 131104 | tf_op jit(solution)/shard_map/ppermute | solution.py:195
  51.3 7.3 %all-to-all-start.1 = ((f32[32,8,128]{2,1,0:T(8,128)}), f32[32,8,128]{2,1,0:T(8,128)S(1)}, u32[]{:S(2)}, u32[]{:S(2)}) async-start(f32[32,8,128]{2,1,0:T(8,128)} %bitcast.7), calls=%async_computation.1 | async-start | bytes 262144 | tf_op jit(solution)/shard_map/all_to_all | solution.py:216
  59.6 8.5 %all-to-all-done.1 = f32[32,8,128]{2,1,0:T(8,128)S(1)} async-done(((f32[32,8,128]{2,1,0:T(8,128)}), f32[32,8,128]{2,1,0:T(8,128)S(1)}, u32[]{:S(2)}, u32[]{:S(2)}) %all-to-all-start.1) | async-done | bytes 131104 | tf_op jit(solution)/shard_map/all_to_all | solution.py:216
  73.9 2.9 %collective-permute-start.17 = (f32[13,8,256]{2,1,0:T(8,128)S(1)}, f32[13,8,256]{2,1,0:T(8,128)S(1)}, u32[]{:S(2)}, u32[]{:S(2)}) collective-permute-start(f32[13,8,256]{2,1,0:T(8,128)S(1)} %get-tuple-element.41), channel_id=1, source_target_pairs={{0,6},{1,7},{2,4},{3,5},{4,2},{5,3},{6,0},{7,1},{8,14},{9,15},{10,... | collective-permute-start | bytes 319496 | tf_op jit(solution)/shard_map/ppermute | solution.py:237
  77.6 4.3 %collective-permute-done.18.far_ref = f32[8,256]{1,0:T(8,128)S(1)} collective-permute-done((f32[8,256]{1,0:T(8,128)S(1)}, f32[8,256]{1,0:T(8,128)S(1)}, u32[]{:S(2)}, u32[]{:S(2)}) %collective-permute-start.18) | collective-permute-done | bytes 8224 | tf_op jit(solution)/shard_map/ppermute | solution.py:236
  85.8 4.6 %collective-permute-done.20.far_ref = f32[8,256]{1,0:T(8,128)S(1)} collective-permute-done((f32[8,256]{1,0:T(8,128)S(1)}, f32[8,256]{1,0:T(8,128)S(1)}, u32[]{:S(2)}, u32[]{:S(2)}) %collective-permute-start.20) | collective-permute-done | bytes 8224 | tf_op jit(solution)/shard_map/ppermute | solution.py:236
  91.4 2.9 %collective-permute-start.21 = (f32[9,8,256]{2,1,0:T(8,128)S(1)}, f32[9,8,256]{2,1,0:T(8,128)S(1)}, u32[]{:S(2)}, u32[]{:S(2)}) collective-permute-start(f32[9,8,256]{2,1,0:T(8,128)S(1)} %get-tuple-element.46), channel_id=1, source_target_pairs={{0,6},{1,7},{2,4},{3,5},{4,2},{5,3},{6,0},{7,1},{8,14},{9,15},{10,... | collective-permute-start | bytes 221192 | tf_op jit(solution)/shard_map/ppermute | solution.py:237
  94.3 5.2 %collective-permute-done.22.far_ref = f32[8,256]{1,0:T(8,128)S(1)} collective-permute-done((f32[8,256]{1,0:T(8,128)S(1)}, f32[8,256]{1,0:T(8,128)S(1)}, u32[]{:S(2)}, u32[]{:S(2)}) %collective-permute-start.22) | collective-permute-done | bytes 8224 | tf_op jit(solution)/shard_map/ppermute | solution.py:236
  100.3 3.9 %collective-permute-start.23 = (f32[7,8,256]{2,1,0:T(8,128)S(1)}, f32[7,8,256]{2,1,0:T(8,128)S(1)}, u32[]{:S(2)}, u32[]{:S(2)}) collective-permute-start(f32[7,8,256]{2,1,0:T(8,128)S(1)} %get-tuple-element.49), channel_id=1, source_target_pairs={{0,30},{1,31},{2,28},{3,29},{4,10},{5,11},{6,8},{7,9},{8,6},{9,7},... | collective-permute-start | bytes 172040 | tf_op jit(solution)/shard_map/ppermute | solution.py:237
  104.2 6.1 %collective-permute-done.24.far_ref = f32[8,256]{1,0:T(8,128)S(1)} collective-permute-done((f32[8,256]{1,0:T(8,128)S(1)}, f32[8,256]{1,0:T(8,128)S(1)}, u32[]{:S(2)}, u32[]{:S(2)}) %collective-permute-start.24) | collective-permute-done | bytes 8224 | tf_op jit(solution)/shard_map/ppermute | solution.py:236
  111.5 5.1 %collective-permute-done.26.far_ref = f32[8,256]{1,0:T(8,128)S(1)} collective-permute-done((f32[8,256]{1,0:T(8,128)S(1)}, f32[8,256]{1,0:T(8,128)S(1)}, u32[]{:S(2)}, u32[]{:S(2)}) %collective-permute-start.26) | collective-permute-done | bytes 8224 | tf_op jit(solution)/shard_map/ppermute | solution.py:236
  117.5 3.2 %collective-permute-start.27 = (f32[3,8,256]{2,1,0:T(8,128)S(1)}, f32[3,8,256]{2,1,0:T(8,128)S(1)}, u32[]{:S(2)}, u32[]{:S(2)}) collective-permute-start(f32[3,8,256]{2,1,0:T(8,128)S(1)} %get-tuple-element.55), channel_id=1, source_target_pairs={{0,30},{1,31},{2,28},{3,29},{4,10},{5,11},{6,8},{7,9},{8,6},{9,7},... | collective-permute-start | bytes 73736 | tf_op jit(solution)/shard_map/ppermute | solution.py:237
  120.7 6.0 %collective-permute-done.28.far_ref = f32[8,256]{1,0:T(8,128)S(1)} collective-permute-done((f32[8,256]{1,0:T(8,128)S(1)}, f32[8,256]{1,0:T(8,128)S(1)}, u32[]{:S(2)}, u32[]{:S(2)}) %collective-permute-start.28) | collective-permute-done | bytes 8224 | tf_op jit(solution)/shard_map/ppermute | solution.py:236
  128.4 3.9 %collective-permute-done.29.near_ref = f32[1,8,256]{2,1,0:T(8,128)S(1)} collective-permute-done((f32[1,8,256]{2,1,0:T(8,128)S(1)}, f32[1,8,256]{2,1,0:T(8,128)S(1)}, u32[]{:S(2)}, u32[]{:S(2)}) %collective-permute-start.29) | collective-permute-done | bytes 8224 | tf_op jit(solution)/shard_map/ppermute | solution.py:237
  134.1 10.4 %all_to_all.15 = f32[8,8,128]{2,1,0:T(8,128)S(1)} all-to-all(f32[8,8,128]{2,1,0:T(8,128)S(1)} %broadcast_in_dim.15), channel_id=1, replica_groups=mesh['row'=8,'quad'=8,'i'=4] {'row'}, dimensions={0} | all-to-all | bytes 65536 | tf_op jit(solution)/shard_map/all_to_all | solution.py:245
  (70 shorter events, 24.3 us)
Async XLA Ops:
  5.7 43.7 %all-to-all-start = ((f32[32,64,128]{2,1,0:T(8,128)}), f32[32,64,128]{2,1,0:T(8,128)}, u32[]{:S(2)}, u32[]{:S(2)}) async-start(f32[32,64,128]{2,1,0:T(8,128)} %shard_map.46), calls=%async_computation | async-start | bytes 2097152 | tf_op jit(solution)/shard_map/all_to_all | solution.py:201
  14.7 18.3 %collective-permute-start.2 = (f32[128,512]{1,0:T(8,128)S(1)}, f32[128,512]{1,0:T(8,128)S(1)}, u32[]{:S(2)}, u32[]{:S(2)}) collective-permute-start(f32[128,512]{1,0:T(8,128)S(1)} %fusion.refs_0_), channel_id=1, source_target_pairs={{0,192},{32,224},{64,0},{96,32},{128,64},{160,96},{192,128},{224,1... | collective-permute-start | bytes 786440 | tf_op jit(solution)/shard_map/ppermute | solution.py:195
  21.0 16.7 %collective-permute-start = (f32[128,512]{1,0:T(8,128)S(1)}, f32[128,512]{1,0:T(8,128)S(1)}, u32[]{:S(2)}, u32[]{:S(2)}) collective-permute-start(f32[128,512]{1,0:T(8,128)S(1)} %fusion.refs_0_), channel_id=1, source_target_pairs={{0,64},{32,96},{64,128},{96,160},{128,192},{160,224},{192,0},{224,... | collective-permute-start | bytes 786440 | tf_op jit(solution)/shard_map/ppermute | solution.py:195
  21.0 18.8 %collective-permute-start.7 = (f32[128,512]{1,0:T(8,128)S(1)}, f32[128,512]{1,0:T(8,128)S(1)}, u32[]{:S(2)}, u32[]{:S(2)}) collective-permute-start(f32[128,512]{1,0:T(8,128)S(1)} %fusion.refs_0_), channel_id=1, source_target_pairs={{0,224},{32,0},{64,32},{96,64},{128,96},{160,128},{192,160},{224,1... | collective-permute-start | bytes 786440 | tf_op jit(solution)/shard_map/ppermute | solution.py:195
  24.7 17.8 %collective-permute-start.6 = (f32[128,512]{1,0:T(8,128)S(1)}, f32[128,512]{1,0:T(8,128)S(1)}, u32[]{:S(2)}, u32[]{:S(2)}) collective-permute-start(f32[128,512]{1,0:T(8,128)S(1)} %fusion.refs_0_), channel_id=1, source_target_pairs={{0,32},{32,64},{64,96},{96,128},{128,160},{160,192},{192,224},{224... | collective-permute-start | bytes 786440 | tf_op jit(solution)/shard_map/ppermute | solution.py:195
  32.9 26.2 %collective-permute-start.5 = (f32[128,512]{1,0:T(8,128)S(1)}, f32[128,512]{1,0:T(8,128)S(1)}, u32[]{:S(2)}, u32[]{:S(2)}) collective-permute-start(f32[128,512]{1,0:T(8,128)S(1)} %collective-permute-done.2.refs_2_), channel_id=1, source_target_pairs={{0,224},{32,0},{64,32},{96,64},{128,96},{160,128},{192,160},{224,1... | collective-permute-start | bytes 786440 | tf_op jit(solution)/shard_map/ppermute | solution.py:195
  35.6 13.8 %collective-permute-start.3 = (f32[64,512]{1,0:T(8,128)S(1)}, f32[64,512]{1,0:T(8,128)}, u32[]{:S(2)}, u32[]{:S(2)}) collective-permute-start(f32[64,512]{1,0:T(8,128)S(1)} %slice.17), channel_id=1, source_target_pairs={{0,192},{32,224},{64,0},{96,32},{128,64},{160,96},{192,128},{224,1... | collective-permute-start | bytes 393224 | tf_op jit(solution)/shard_map/ppermute | solution.py:195
  37.8 21.6 %collective-permute-start.4 = (f32[128,512]{1,0:T(8,128)S(1)}, f32[128,512]{1,0:T(8,128)S(1)}, u32[]{:S(2)}, u32[]{:S(2)}) collective-permute-start(f32[128,512]{1,0:T(8,128)S(1)} %collective-permute-done.refs_1_), channel_id=1, source_target_pairs={{0,32},{32,64},{64,96},{96,128},{128,160},{160,192},{192,224},{224... | collective-permute-start | bytes 786440 | tf_op jit(solution)/shard_map/ppermute | solution.py:195
  39.9 18.8 %collective-permute-start.1 = (f32[64,512]{1,0:T(8,128)S(1)}, f32[64,512]{1,0:T(8,128)}, u32[]{:S(2)}, u32[]{:S(2)}) collective-permute-start(f32[64,512]{1,0:T(8,128)S(1)} %slice.16), channel_id=1, source_target_pairs={{0,64},{32,96},{64,128},{96,160},{128,192},{160,224},{192,0},{224,... | collective-permute-start | bytes 393224 | tf_op jit(solution)/shard_map/ppermute | solution.py:195
  42.5 25.6 %collective-permute-start.8 = (f32[128,512]{1,0:T(8,128)S(1)}, f32[128,512]{1,0:T(8,128)S(1)}, u32[]{:S(2)}, u32[]{:S(2)}) collective-permute-start(f32[128,512]{1,0:T(8,128)S(1)} %fusion.refs_0_), channel_id=1, source_target_pairs={{0,1},{1,0},{2,3},{3,2},{4,5},{5,4},{6,7},{7,6},{8,9},{9,8},{10,11... | collective-permute-start | bytes 786440 | tf_op jit(solution)/shard_map/ppermute | solution.py:212
  49.4 18.8 %collective-permute-start.12 = (f32[128,512]{1,0:T(8,128)S(1)}, f32[128,512]{1,0:T(8,128)S(1)}, u32[]{:S(2)}, u32[]{:S(2)}) collective-permute-start(f32[128,512]{1,0:T(8,128)S(1)} %collective-permute-done.7.refs_4_), channel_id=1, source_target_pairs={{0,1},{1,0},{2,3},{3,2},{4,5},{5,4},{6,7},{7,6},{8,9},{9,8},{10,11... | collective-permute-start | bytes 786440 | tf_op jit(solution)/shard_map/ppermute | solution.py:212
  51.3 16.8 %all-to-all-start.1 = ((f32[32,8,128]{2,1,0:T(8,128)}), f32[32,8,128]{2,1,0:T(8,128)S(1)}, u32[]{:S(2)}, u32[]{:S(2)}) async-start(f32[32,8,128]{2,1,0:T(8,128)} %bitcast.7), calls=%async_computation.1 | async-start | bytes 262144 | tf_op jit(solution)/shard_map/all_to_all | solution.py:216
  58.7 9.9 %collective-permute-start.11 = (f32[128,512]{1,0:T(8,128)S(1)}, f32[128,512]{1,0:T(8,128)S(1)}, u32[]{:S(2)}, u32[]{:S(2)}) collective-permute-start(f32[128,512]{1,0:T(8,128)S(1)} %collective-permute-done.6.refs_3_), channel_id=1, source_target_pairs={{0,1},{1,0},{2,3},{3,2},{4,5},{5,4},{6,7},{7,6},{8,9},{9,8},{10,11... | collective-permute-start | bytes 786440 | tf_op jit(solution)/shard_map/ppermute | solution.py:212
  59.1 9.9 %collective-permute-start.10 = (f32[128,512]{1,0:T(8,128)S(1)}, f32[128,512]{1,0:T(8,128)S(1)}, u32[]{:S(2)}, u32[]{:S(2)}) collective-permute-start(f32[128,512]{1,0:T(8,128)S(1)} %collective-permute-done.2.refs_2_), channel_id=1, source_target_pairs={{0,1},{1,0},{2,3},{3,2},{4,5},{5,4},{6,7},{7,6},{8,9},{9,8},{10,11... | collective-permute-start | bytes 786440 | tf_op jit(solution)/shard_map/ppermute | solution.py:212
  59.3 9.9 %collective-permute-start.9 = (f32[128,512]{1,0:T(8,128)S(1)}, f32[128,512]{1,0:T(8,128)S(1)}, u32[]{:S(2)}, u32[]{:S(2)}) collective-permute-start(f32[128,512]{1,0:T(8,128)S(1)} %collective-permute-done.refs_1_), channel_id=1, source_target_pairs={{0,1},{1,0},{2,3},{3,2},{4,5},{5,4},{6,7},{7,6},{8,9},{9,8},{10,11... | collective-permute-start | bytes 786440 | tf_op jit(solution)/shard_map/ppermute | solution.py:212
  73.9 8.0 %collective-permute-start.17 = (f32[13,8,256]{2,1,0:T(8,128)S(1)}, f32[13,8,256]{2,1,0:T(8,128)S(1)}, u32[]{:S(2)}, u32[]{:S(2)}) collective-permute-start(f32[13,8,256]{2,1,0:T(8,128)S(1)} %get-tuple-element.41), channel_id=1, source_target_pairs={{0,6},{1,7},{2,4},{3,5},{4,2},{5,3},{6,0},{7,1},{8,14},{9,15},{10,... | collective-permute-start | bytes 319496 | tf_op jit(solution)/shard_map/ppermute | solution.py:237
  83.0 7.5 %collective-permute-start.19 = (f32[11,8,256]{2,1,0:T(8,128)S(1)}, f32[11,8,256]{2,1,0:T(8,128)S(1)}, u32[]{:S(2)}, u32[]{:S(2)}) collective-permute-start(f32[11,8,256]{2,1,0:T(8,128)S(1)} %get-tuple-element.43), channel_id=1, source_target_pairs={{0,30},{1,31},{2,28},{3,29},{4,10},{5,11},{6,8},{7,9},{8,6},{9,7},... | collective-permute-start | bytes 270344 | tf_op jit(solution)/shard_map/ppermute | solution.py:237
  84.4 6.1 %collective-permute-start.20 = (f32[8,256]{1,0:T(8,128)S(1)}, f32[8,256]{1,0:T(8,128)S(1)}, u32[]{:S(2)}, u32[]{:S(2)}) collective-permute-start(f32[8,256]{1,0:T(8,128)S(1)} %get-tuple-element.44), channel_id=1, source_target_pairs={{0,28},{1,29},{2,30},{3,31},{4,8},{5,9},{6,10},{7,11},{8,4},{9,5},... | collective-permute-start | bytes 24584 | tf_op jit(solution)/shard_map/ppermute | solution.py:236
  91.4 8.1 %collective-permute-start.21 = (f32[9,8,256]{2,1,0:T(8,128)S(1)}, f32[9,8,256]{2,1,0:T(8,128)S(1)}, u32[]{:S(2)}, u32[]{:S(2)}) collective-permute-start(f32[9,8,256]{2,1,0:T(8,128)S(1)} %get-tuple-element.46), channel_id=1, source_target_pairs={{0,6},{1,7},{2,4},{3,5},{4,2},{5,3},{6,0},{7,1},{8,14},{9,15},{10,... | collective-permute-start | bytes 221192 | tf_op jit(solution)/shard_map/ppermute | solution.py:237
  100.3 10.0 %collective-permute-start.23 = (f32[7,8,256]{2,1,0:T(8,128)S(1)}, f32[7,8,256]{2,1,0:T(8,128)S(1)}, u32[]{:S(2)}, u32[]{:S(2)}) collective-permute-start(f32[7,8,256]{2,1,0:T(8,128)S(1)} %get-tuple-element.49), channel_id=1, source_target_pairs={{0,30},{1,31},{2,28},{3,29},{4,10},{5,11},{6,8},{7,9},{8,6},{9,7},... | collective-permute-start | bytes 172040 | tf_op jit(solution)/shard_map/ppermute | solution.py:237
  104.2 6.1 %collective-permute-start.24 = (f32[8,256]{1,0:T(8,128)S(1)}, f32[8,256]{1,0:T(8,128)S(1)}, u32[]{:S(2)}, u32[]{:S(2)}) collective-permute-start(f32[8,256]{1,0:T(8,128)S(1)} %get-tuple-element.50), channel_id=1, source_target_pairs={{0,28},{1,29},{2,30},{3,31},{4,8},{5,9},{6,10},{7,11},{8,4},{9,5},... | collective-permute-start | bytes 24584 | tf_op jit(solution)/shard_map/ppermute | solution.py:236
  111.1 5.6 %collective-permute-start.25 = (f32[5,8,256]{2,1,0:T(8,128)S(1)}, f32[5,8,256]{2,1,0:T(8,128)S(1)}, u32[]{:S(2)}, u32[]{:S(2)}) collective-permute-start(f32[5,8,256]{2,1,0:T(8,128)S(1)} %get-tuple-element.52), channel_id=1, source_target_pairs={{0,6},{1,7},{2,4},{3,5},{4,2},{5,3},{6,0},{7,1},{8,14},{9,15},{10,... | collective-permute-start | bytes 122888 | tf_op jit(solution)/shard_map/ppermute | solution.py:237
  117.5 9.2 %collective-permute-start.27 = (f32[3,8,256]{2,1,0:T(8,128)S(1)}, f32[3,8,256]{2,1,0:T(8,128)S(1)}, u32[]{:S(2)}, u32[]{:S(2)}) collective-permute-start(f32[3,8,256]{2,1,0:T(8,128)S(1)} %get-tuple-element.55), channel_id=1, source_target_pairs={{0,30},{1,31},{2,28},{3,29},{4,10},{5,11},{6,8},{7,9},{8,6},{9,7},... | collective-permute-start | bytes 73736 | tf_op jit(solution)/shard_map/ppermute | solution.py:237
  120.7 6.1 %collective-permute-start.28 = (f32[8,256]{1,0:T(8,128)S(1)}, f32[8,256]{1,0:T(8,128)S(1)}, u32[]{:S(2)}, u32[]{:S(2)}) collective-permute-start(f32[8,256]{1,0:T(8,128)S(1)} %get-tuple-element.56), channel_id=1, source_target_pairs={{0,28},{1,29},{2,30},{3,31},{4,8},{5,9},{6,10},{7,11},{8,4},{9,5},... | collective-permute-start | bytes 24584 | tf_op jit(solution)/shard_map/ppermute | solution.py:236
  (13 other events, 60.8 us)
where the time goes:
time: 147 us; the launch traced here: 145 us
  waiting for transfers between devices  64.2 us (44%)
  starting transfers between devices  51.9 us (35%)
  Pallas kernels  12.9 us (9%)
  blocking collectives  10.4 us (7%)
  local copies, waits for them, and re-layouts  2.97 us (2%)
    ppermute x7, waiting for transfers between devices, solve(): far = lax.ppermute(same, ('quad', 'i'), far_to)  32.5 us
    ppermute x8, waiting for transfers between devices, shift(): lax.ppermute(shard, 'row', [(r, (r + by) % rows) for r in range(rows)])  17.7 us
    ppermute x8, starting transfers between devices, shift(): lax.ppermute(shard, 'row', [(r, (r + by) % rows) for r in range(rows)])  17 us
    ppermute x7, starting transfers between devices, solve(): got = lax.ppermute(sent, ('quad', 'i'), near_to)  15.4 us
    all_to_all x1, blocking collectives, solve(): lax.all_to_all(jnp.broadcast_to(final[None], (rows, group, piece_len)), '...  10.4 us
    all_to_all x1, waiting for transfers between devices, solve(): incoming = lax.all_to_all(outgoing, ('row', 'i'), 0, 0, tiled=True)  8.55 us
    all_to_all x1, starting transfers between devices, solve(): spread = lax.all_to_all(taken, ('quad', 'i'), 0, 0, tiled=True)  7.68 us
    all_to_all x1, starting transfers between devices, solve(): incoming = lax.all_to_all(outgoing, ('row', 'i'), 0, 0, tiled=True)  7.34 us
  transfers between devices with their start and end apart: 33, of which 15 were waited for; matrix products, arithmetic and copies ran while one was open for 2% of the time, Pallas kernels for 0%

commit v1 on v0

--- a/solution.py
+++ b/solution.py
@@ -133,6 +133,7 @@
 
 def first_kernel(flags_ref, pieces_ref, hi_ref, mid_ref, start_ref, same_ref, sent_ref):
     sums = jnp.sum(pieces_ref[...], axis=0)
+    sums = jnp.where(flags_ref[4] == 1, jnp.concatenate([sums[2:], sums[:2]], axis=0), sums)
     block = jnp.concatenate([sums[i] for i in range(QUAD)], axis=1)
     own = flags_ref[2]
     start = product(block, hi_ref[own], mid_ref[own], NT)
@@ -162,10 +163,18 @@
     )(flags, *args)
 
 
+def mirrored(quad, i):
+    if quad // 2 % 2:
+        return quad, i
+    return quad ^ 1, i ^ 2
+
+
 def next_quad(quad, step, quads):
     if step % 2 == 0:
         return quad ^ 1
-    return (quad + (1 if quad % 2 else -1)) % quads
+    turn, side = quad // 2, quad % 2
+    turn = turn ^ 1 if step % 4 == 1 else (turn + 1 if turn % 2 else turn - 1) % (quads // 2)
+    return 2 * turn + side
 
 
 def solve(rhs, pivots, factor, diag_inv):
@@ -174,8 +183,11 @@
     my_i = lax.axis_index("i")
     rows = lax.axis_size("row")
     quads = lax.axis_size("quad")
-    core = my_i % 2
-    half = my_i // 2
+    turned = my_quad // 2 % 2 == 0
+    at_quad = jnp.where(turned, my_quad ^ 1, my_quad)
+    at_i = jnp.where(turned, my_i ^ 2, my_i)
+    core = at_i % 2
+    half = at_i // 2
     rhs_count, source_len = rhs.shape
     block_len, _, _, piece_len = factor.shape
     group = rhs_count // rows
@@ -185,11 +197,19 @@
     def pairs(move):
         return [(q * QUAD + i, move(q, i)[0] * QUAD + move(q, i)[1]) for q, i in places]
 
-    lower = factor.reshape(block_len, piece_len)
+    def mirror(shard):
+        there = [(a, b) for a, b in pairs(mirrored) if a != b]
+        return jnp.where(turned, lax.ppermute(shard, ("quad", "i"), there), shard)
+
+    lower = mirror(factor.reshape(block_len, piece_len))
+    order = pivots.reshape(quads // 2, 4, -1)
+    even = lax.broadcasted_iota(jnp.int32, order.shape, 0) % 2 == 0
+    order = jnp.where(even, order[:, ::-1], order).reshape(-1)
+    taken = take_columns(rhs, order, flat * source_len, piece_len)
     inverse = diag_inv[0]
     scaled = dot(lower, inverse, ((0,), (1,)))
-    own_rows = lax.dynamic_slice_in_dim(inverse, my_i * piece_len, piece_len, 0)
-    slot = jnp.where(my_quad == my_row, own_rows, -scaled)
+    own_rows = lax.dynamic_slice_in_dim(inverse, at_i * piece_len, piece_len, 0)
+    slot = jnp.where(at_quad == my_row, own_rows, -scaled)
 
     def shift(shard, by):
         return lax.ppermute(shard, "row", [(r, (r + by) % rows) for r in range(rows)])
@@ -197,7 +217,6 @@
     partner = [(i, i ^ 1) for i in range(QUAD)]
     first = [shift(slot, 2), shift(slot, -2)]
     first += [shift(slot, 1), shift(slot, -1)]
-    taken = take_columns(rhs, pivots, flat * source_len, piece_len)
     spread = lax.all_to_all(taken, ("quad", "i"), 0, 0, tiled=True)
     piece = spread.sum(axis=0)
     cut = piece_len // 2
@@ -216,7 +235,7 @@
     incoming = lax.all_to_all(outgoing, ("row", "i"), 0, 0, tiled=True)
     incoming, *second = lax.optimization_barrier((incoming, *second))
     theirs += [lax.ppermute(rows_of, "i", partner) for rows_of in second]
-    flags = jnp.stack([core, half, my_quad, my_row]).astype(jnp.int32)
+    flags = jnp.stack([core, half, at_quad, my_row, turned.astype(jnp.int32)]).astype(jnp.int32)
     hi, mid = prepare(flags, rows, parts, near_rows + second, theirs)
     wide = (group, 2 * piece_len)
 
@@ -231,8 +250,9 @@
     )
     final = start
     for step in range(quads - 1):
-        far_to = pairs(lambda q, i: (next_quad(q, step, quads), i))
-        near_to = pairs(lambda q, i: (next_quad(q, step, quads), i ^ 2))
+        near = 2 if step % 2 == 0 else 0
+        far_to = pairs(lambda q, i: (next_quad(q, step, quads), i ^ 2 ^ near))
+        near_to = pairs(lambda q, i: (next_quad(q, step, quads), i ^ near))
         far = lax.ppermute(same, ("quad", "i"), far_to)
         got = lax.ppermute(sent, ("quad", "i"), near_to)
         args, outs = (start, got, far, final), (wide,)
@@ -241,6 +261,9 @@
         final, *rest = call(functools.partial(step_kernel, step + 1), flags, args, outs)
         if rest:
             same, sent = rest
+        if step == quads - 4:
+            home = mirror(final)
+    final = jnp.where(turned, home, final)
     final = jnp.where(core == 0, final[:, :piece_len], final[:, piece_len:])
     whole = lax.all_to_all(
         jnp.broadcast_to(final[None], (rows, group, piece_len)), "row", 0, 0, tiled=True

time: 147 us -> 156 us (1.061)
  starting transfers between devices: 51.9 us -> 69.5 us
  waiting for transfers between devices: 64.2 us -> 57.2 us
    ppermute x7, starting transfers between devices: 15.4 us -> 30.9 us  [solve(): got = lax.ppermute(sent, ('quad', 'i'), near_to)]
    ppermute x7, waiting for transfers between devices: 32.5 us -> 27.8 us  [solve(): far = lax.ppermute(same, ('quad', 'i'), far_to)]
    ppermute x7, waiting for transfers between devices: 4.08 us -> 2.36 us  [solve(): got = lax.ppermute(sent, ('quad', 'i'), near_to)]
  transfers between devices with their start and end apart: 33 -> 35, of which waited for: 15 -> 14; matrix products, arithmetic and copies ran while one was open for 2% -> 2% of each run, Pallas kernels for 0% -> 0%
where the time goes in v1:
time: 156 us
  starting transfers between devices  69.5 us (45%)
  waiting for transfers between devices  57.2 us (37%)
  Pallas kernels  12.8 us (8%)
  blocking collectives  10.6 us (7%)
  local copies, waits for them, and re-layouts  3.81 us (2%)
    ppermute x7, starting transfers between devices, solve(): got = lax.ppermute(sent, ('quad', 'i'), near_to)  30.9 us
    ppermute x7, waiting for transfers between devices, solve(): far = lax.ppermute(same, ('quad', 'i'), far_to)  27.8 us
    ppermute x8, waiting for transfers between devices, shift(): lax.ppermute(shard, 'row', [(r, (r + by) % rows) for r in range(rows)])  17.1 us
    ppermute x8, starting transfers between devices, shift(): lax.ppermute(shard, 'row', [(r, (r + by) % rows) for r in range(rows)])  16.9 us
    all_to_all x1, blocking collectives, solve(): lax.all_to_all(jnp.broadcast_to(final[None], (rows, group, piece_len)), '...  10.6 us
    all_to_all x1, waiting for transfers between devices, solve(): incoming = lax.all_to_all(outgoing, ('row', 'i'), 0, 0, tiled=True)  8.55 us
    all_to_all x1, starting transfers between devices, solve(): spread = lax.all_to_all(taken, ('quad', 'i'), 0, 0, tiled=True)  7.62 us
    all_to_all x1, starting transfers between devices, solve(): incoming = lax.all_to_all(outgoing, ('row', 'i'), 0, 0, tiled=True)  7.34 us
  transfers between devices with their start and end apart: 35, of which 14 were waited for; matrix products, arithmetic and copies ran while one was open for 2% of the time, Pallas kernels for 0%

profile of v1, /device:TPU:2, one launch (start us, length us, event | category | flops | bytes accessed | tf_op | source)
XLA Modules:
  0.0 155.6 jit_solution(12061918397092510199)
XLA Ops:
  1.9 4.0 %shard_map.46 = f32[32,64,128]{2,1,0:T(8,128)} custom-call(s32[1]{0:T(128)} %bitcast.5.first_ref, s32[1,4096]{1,0:T(1,128)S(1)} %reshape_reshape.3.pivots_ref, f32[64,512]{1,0:T(8,128)S(1)} %copy-done), custom_call_target="tpu_custom_call" | custom-call | tf_op jit(solution)/shard_map/pallas_call | solution.py:51
  5.9 7.6 %all-to-all-start = ((f32[32,64,128]{2,1,0:T(8,128)}), f32[32,64,128]{2,1,0:T(8,128)S(1)}, u32[]{:S(2)}, u32[]{:S(2)}) async-start(f32[32,64,128]{2,1,0:T(8,128)} %shard_map.46), calls=%async_computation | async-start | bytes 2097152 | tf_op jit(solution)/shard_map/all_to_all | solution.py:220
  15.6 6.4 %collective-permute-start.3 = (f32[128,512]{1,0:T(8,128)S(1)}, f32[128,512]{1,0:T(8,128)S(1)}, u32[]{:S(2)}, u32[]{:S(2)}) collective-permute-start(f32[128,512]{1,0:T(8,128)S(1)} %fusion.refs_0_), channel_id=1, source_target_pairs={{0,192},{32,224},{64,0},{96,32},{128,64},{160,96},{192,128},{224,1... | collective-permute-start | bytes 786440 | tf_op jit(solution)/shard_map/ppermute | solution.py:215
  21.9 3.7 %collective-permute-start.8 = (f32[128,512]{1,0:T(8,128)S(1)}, f32[128,512]{1,0:T(8,128)S(1)}, u32[]{:S(2)}, u32[]{:S(2)}) collective-permute-start(f32[128,512]{1,0:T(8,128)S(1)} %fusion.refs_0_), channel_id=1, source_target_pairs={{0,224},{32,0},{64,32},{96,64},{128,96},{160,128},{192,160},{224,1... | collective-permute-start | bytes 786440 | tf_op jit(solution)/shard_map/ppermute | solution.py:215
  25.6 8.2 %collective-permute-done.3.refs_2_ = f32[128,512]{1,0:T(8,128)S(1)} collective-permute-done((f32[128,512]{1,0:T(8,128)S(1)}, f32[128,512]{1,0:T(8,128)S(1)}, u32[]{:S(2)}, u32[]{:S(2)}) %collective-permute-start.3) | collective-permute-done | bytes 262176 | tf_op jit(solution)/shard_map/ppermute | solution.py:215
  33.8 2.7 %collective-permute-start.6 = (f32[128,512]{1,0:T(8,128)S(1)}, f32[128,512]{1,0:T(8,128)S(1)}, u32[]{:S(2)}, u32[]{:S(2)}) collective-permute-start(f32[128,512]{1,0:T(8,128)S(1)} %collective-permute-done.3.refs_2_), channel_id=1, source_target_pairs={{0,224},{32,0},{64,32},{96,64},{128,96},{160,128},{192,160},{224,1... | collective-permute-start | bytes 786440 | tf_op jit(solution)/shard_map/ppermute | solution.py:215
  36.5 2.1 %collective-permute-start.4 = (f32[64,512]{1,0:T(8,128)S(1)}, f32[64,512]{1,0:T(8,128)}, u32[]{:S(2)}, u32[]{:S(2)}) collective-permute-start(f32[64,512]{1,0:T(8,128)S(1)} %slice.17), channel_id=1, source_target_pairs={{0,192},{32,224},{64,0},{96,32},{128,64},{160,96},{192,128},{224,1... | collective-permute-start | bytes 393224 | tf_op jit(solution)/shard_map/ppermute | solution.py:215
  38.7 2.0 %collective-permute-start.5 = (f32[128,512]{1,0:T(8,128)S(1)}, f32[128,512]{1,0:T(8,128)S(1)}, u32[]{:S(2)}, u32[]{:S(2)}) collective-permute-start(f32[128,512]{1,0:T(8,128)S(1)} %collective-permute-done.1.refs_1_), channel_id=1, source_target_pairs={{0,32},{32,64},{64,96},{96,128},{128,160},{160,192},{192,224},{224... | collective-permute-start | bytes 786440 | tf_op jit(solution)/shard_map/ppermute | solution.py:215
  41.4 2.1 %collective-permute-done.7.refs_3_ = f32[128,512]{1,0:T(8,128)S(1)} collective-permute-done((f32[128,512]{1,0:T(8,128)S(1)}, f32[128,512]{1,0:T(8,128)S(1)}, u32[]{:S(2)}, u32[]{:S(2)}) %collective-permute-start.7) | collective-permute-done | bytes 262176 | tf_op jit(solution)/shard_map/ppermute | solution.py:215
  43.4 6.9 %collective-permute-done.4.refs_6_ = f32[64,512]{1,0:T(8,128)} collective-permute-done((f32[64,512]{1,0:T(8,128)S(1)}, f32[64,512]{1,0:T(8,128)}, u32[]{:S(2)}, u32[]{:S(2)}) %collective-permute-start.4) | collective-permute-done | bytes 131104 | tf_op jit(solution)/shard_map/ppermute | solution.py:215
  51.0 7.3 %all-to-all-start.1 = ((f32[32,8,128]{2,1,0:T(8,128)}), f32[32,8,128]{2,1,0:T(8,128)S(1)}, u32[]{:S(2)}, u32[]{:S(2)}) async-start(f32[32,8,128]{2,1,0:T(8,128)} %bitcast.7), calls=%async_computation.1 | async-start | bytes 262144 | tf_op jit(solution)/shard_map/all_to_all | solution.py:235
  59.3 8.5 %all-to-all-done.1 = f32[32,8,128]{2,1,0:T(8,128)S(1)} async-done(((f32[32,8,128]{2,1,0:T(8,128)}), f32[32,8,128]{2,1,0:T(8,128)S(1)}, u32[]{:S(2)}, u32[]{:S(2)}) %all-to-all-start.1) | async-done | bytes 131104 | tf_op jit(solution)/shard_map/all_to_all | solution.py:235
  73.5 2.9 %collective-permute-start.18 = (f32[13,8,256]{2,1,0:T(8,128)S(1)}, f32[13,8,256]{2,1,0:T(8,128)S(1)}, u32[]{:S(2)}, u32[]{:S(2)}) collective-permute-start(f32[13,8,256]{2,1,0:T(8,128)S(1)} %get-tuple-element.41), channel_id=1, source_target_pairs={{0,6},{1,7},{2,4},{3,5},{4,2},{5,3},{6,0},{7,1},{8,14},{9,15},{10,... | collective-permute-start | bytes 319496 | tf_op jit(solution)/shard_map/ppermute | solution.py:257
  77.2 4.3 %collective-permute-done.19.far_ref = f32[8,256]{1,0:T(8,128)S(1)} collective-permute-done((f32[8,256]{1,0:T(8,128)S(1)}, f32[8,256]{1,0:T(8,128)S(1)}, u32[]{:S(2)}, u32[]{:S(2)}) %collective-permute-start.19) | collective-permute-done | bytes 8224 | tf_op jit(solution)/shard_map/ppermute | solution.py:256
  82.6 18.4 %collective-permute-start.20 = (f32[11,8,256]{2,1,0:T(8,128)S(1)}, f32[11,8,256]{2,1,0:T(8,128)S(1)}, u32[]{:S(2)}, u32[]{:S(2)}) collective-permute-start(f32[11,8,256]{2,1,0:T(8,128)S(1)} %get-tuple-element.43), channel_id=1, source_target_pairs={{0,8},{1,9},{2,10},{3,11},{4,12},{5,13},{6,14},{7,15},{8,0},{9,1},... | collective-permute-start | bytes 270344 | tf_op jit(solution)/shard_map/ppermute | solution.py:257
  101.0 4.5 %collective-permute-done.21.far_ref = f32[8,256]{1,0:T(8,128)S(1)} collective-permute-done((f32[8,256]{1,0:T(8,128)S(1)}, f32[8,256]{1,0:T(8,128)S(1)}, u32[]{:S(2)}, u32[]{:S(2)}) %collective-permute-start.21) | collective-permute-done | bytes 8224 | tf_op jit(solution)/shard_map/ppermute | solution.py:256
  108.5 4.6 %collective-permute-done.23.far_ref = f32[8,256]{1,0:T(8,128)S(1)} collective-permute-done((f32[8,256]{1,0:T(8,128)S(1)}, f32[8,256]{1,0:T(8,128)S(1)}, u32[]{:S(2)}, u32[]{:S(2)}) %collective-permute-start.23) | collective-permute-done | bytes 8224 | tf_op jit(solution)/shard_map/ppermute | solution.py:256
  115.9 4.0 %collective-permute-done.25.far_ref = f32[8,256]{1,0:T(8,128)S(1)} collective-permute-done((f32[8,256]{1,0:T(8,128)S(1)}, f32[8,256]{1,0:T(8,128)S(1)}, u32[]{:S(2)}, u32[]{:S(2)}) %collective-permute-start.25) | collective-permute-done | bytes 8224 | tf_op jit(solution)/shard_map/ppermute | solution.py:256
  123.3 3.7 %collective-permute-done.27.far_ref = f32[8,256]{1,0:T(8,128)S(1)} collective-permute-done((f32[8,256]{1,0:T(8,128)S(1)}, f32[8,256]{1,0:T(8,128)S(1)}, u32[]{:S(2)}, u32[]{:S(2)}) %collective-permute-start.27) | collective-permute-done | bytes 8224 | tf_op jit(solution)/shard_map/ppermute | solution.py:256
  127.7 3.8 %collective-permute-start.29 = (f32[3,8,256]{2,1,0:T(8,128)S(1)}, f32[3,8,256]{2,1,0:T(8,128)S(1)}, u32[]{:S(2)}, u32[]{:S(2)}) collective-permute-start(f32[3,8,256]{2,1,0:T(8,128)S(1)} %get-tuple-element.56), channel_id=1, source_target_pairs={{0,8},{1,9},{2,10},{3,11},{4,12},{5,13},{6,14},{7,15},{8,0},{9,1},... | collective-permute-start | bytes 73736 | tf_op jit(solution)/shard_map/ppermute | solution.py:257
  131.5 4.5 %collective-permute-done.30.far_ref = f32[8,256]{1,0:T(8,128)S(1)} collective-permute-done((f32[8,256]{1,0:T(8,128)S(1)}, f32[8,256]{1,0:T(8,128)S(1)}, u32[]{:S(2)}, u32[]{:S(2)}) %collective-permute-start.30) | collective-permute-done | bytes 8224 | tf_op jit(solution)/shard_map/ppermute | solution.py:256
  139.3 2.3 %collective-permute-done.31.near_ref = f32[1,8,256]{2,1,0:T(8,128)S(1)} collective-permute-done((f32[1,8,256]{2,1,0:T(8,128)S(1)}, f32[1,8,256]{2,1,0:T(8,128)S(1)}, u32[]{:S(2)}, u32[]{:S(2)}) %collective-permute-start.31) | collective-permute-done | bytes 8224 | tf_op jit(solution)/shard_map/ppermute | solution.py:257
  141.7 2.1 %collective-permute-done.32.far_ref = f32[8,256]{1,0:T(8,128)S(1)} collective-permute-done((f32[8,256]{1,0:T(8,128)S(1)}, f32[8,256]{1,0:T(8,128)S(1)}, u32[]{:S(2)}, u32[]{:S(2)}) %collective-permute-start.32) | collective-permute-done | bytes 8224 | tf_op jit(solution)/shard_map/ppermute | solution.py:256
  144.4 10.6 %all_to_all.15 = f32[8,8,128]{2,1,0:T(8,128)S(1)} all-to-all(f32[8,8,128]{2,1,0:T(8,128)S(1)} %broadcast_in_dim.15), channel_id=1, replica_groups=mesh['row'=8,'quad'=8,'i'=4] {'row'}, dimensions={0} | all-to-all | bytes 65536 | tf_op jit(solution)/shard_map/all_to_all | solution.py:268
  (79 shorter events, 27.9 us)
Async XLA Ops:
  5.9 44.4 %all-to-all-start = ((f32[32,64,128]{2,1,0:T(8,128)}), f32[32,64,128]{2,1,0:T(8,128)S(1)}, u32[]{:S(2)}, u32[]{:S(2)}) async-start(f32[32,64,128]{2,1,0:T(8,128)} %shard_map.46), calls=%async_computation | async-start | bytes 2097152 | tf_op jit(solution)/shard_map/all_to_all | solution.py:220
  15.6 18.3 %collective-permute-start.3 = (f32[128,512]{1,0:T(8,128)S(1)}, f32[128,512]{1,0:T(8,128)S(1)}, u32[]{:S(2)}, u32[]{:S(2)}) collective-permute-start(f32[128,512]{1,0:T(8,128)S(1)} %fusion.refs_0_), channel_id=1, source_target_pairs={{0,192},{32,224},{64,0},{96,32},{128,64},{160,96},{192,128},{224,1... | collective-permute-start | bytes 786440 | tf_op jit(solution)/shard_map/ppermute | solution.py:215
  21.9 16.7 %collective-permute-start.1 = (f32[128,512]{1,0:T(8,128)S(1)}, f32[128,512]{1,0:T(8,128)S(1)}, u32[]{:S(2)}, u32[]{:S(2)}) collective-permute-start(f32[128,512]{1,0:T(8,128)S(1)} %fusion.refs_0_), channel_id=1, source_target_pairs={{0,64},{32,96},{64,128},{96,160},{128,192},{160,224},{192,0},{224,... | collective-permute-start | bytes 786440 | tf_op jit(solution)/shard_map/ppermute | solution.py:215
  21.9 19.4 %collective-permute-start.8 = (f32[128,512]{1,0:T(8,128)S(1)}, f32[128,512]{1,0:T(8,128)S(1)}, u32[]{:S(2)}, u32[]{:S(2)}) collective-permute-start(f32[128,512]{1,0:T(8,128)S(1)} %fusion.refs_0_), channel_id=1, source_target_pairs={{0,224},{32,0},{64,32},{96,64},{128,96},{160,128},{192,160},{224,1... | collective-permute-start | bytes 786440 | tf_op jit(solution)/shard_map/ppermute | solution.py:215
  25.6 17.8 %collective-permute-start.7 = (f32[128,512]{1,0:T(8,128)S(1)}, f32[128,512]{1,0:T(8,128)S(1)}, u32[]{:S(2)}, u32[]{:S(2)}) collective-permute-start(f32[128,512]{1,0:T(8,128)S(1)} %fusion.refs_0_), channel_id=1, source_target_pairs={{0,32},{32,64},{64,96},{96,128},{128,160},{160,192},{192,224},{224... | collective-permute-start | bytes 786440 | tf_op jit(solution)/shard_map/ppermute | solution.py:215
  33.8 24.9 %collective-permute-start.6 = (f32[128,512]{1,0:T(8,128)S(1)}, f32[128,512]{1,0:T(8,128)S(1)}, u32[]{:S(2)}, u32[]{:S(2)}) collective-permute-start(f32[128,512]{1,0:T(8,128)S(1)} %collective-permute-done.3.refs_2_), channel_id=1, source_target_pairs={{0,224},{32,0},{64,32},{96,64},{128,96},{160,128},{192,160},{224,1... | collective-permute-start | bytes 786440 | tf_op jit(solution)/shard_map/ppermute | solution.py:215
  36.5 13.8 %collective-permute-start.4 = (f32[64,512]{1,0:T(8,128)S(1)}, f32[64,512]{1,0:T(8,128)}, u32[]{:S(2)}, u32[]{:S(2)}) collective-permute-start(f32[64,512]{1,0:T(8,128)S(1)} %slice.17), channel_id=1, source_target_pairs={{0,192},{32,224},{64,0},{96,32},{128,64},{160,96},{192,128},{224,1... | collective-permute-start | bytes 393224 | tf_op jit(solution)/shard_map/ppermute | solution.py:215
  38.7 20.3 %collective-permute-start.5 = (f32[128,512]{1,0:T(8,128)S(1)}, f32[128,512]{1,0:T(8,128)S(1)}, u32[]{:S(2)}, u32[]{:S(2)}) collective-permute-start(f32[128,512]{1,0:T(8,128)S(1)} %collective-permute-done.1.refs_1_), channel_id=1, source_target_pairs={{0,32},{32,64},{64,96},{96,128},{128,160},{160,192},{192,224},{224... | collective-permute-start | bytes 786440 | tf_op jit(solution)/shard_map/ppermute | solution.py:215
  41.4 17.0 %collective-permute-start.2 = (f32[64,512]{1,0:T(8,128)}, f32[64,512]{1,0:T(8,128)}, u32[]{:S(2)}, u32[]{:S(2)}) collective-permute-start(f32[64,512]{1,0:T(8,128)} %slice.16), channel_id=1, source_target_pairs={{0,64},{32,96},{64,128},{96,160},{128,192},{160,224},{192,0},{224,... | collective-permute-start | bytes 393224 | tf_op jit(solution)/shard_map/ppermute | solution.py:215
  43.4 24.4 %collective-permute-start.9 = (f32[128,512]{1,0:T(8,128)S(1)}, f32[128,512]{1,0:T(8,128)S(1)}, u32[]{:S(2)}, u32[]{:S(2)}) collective-permute-start(f32[128,512]{1,0:T(8,128)S(1)} %fusion.refs_0_), channel_id=1, source_target_pairs={{0,1},{1,0},{2,3},{3,2},{4,5},{5,4},{6,7},{7,6},{8,9},{9,8},{10,11... | collective-permute-start | bytes 786440 | tf_op jit(solution)/shard_map/ppermute | solution.py:231
  50.3 17.6 %collective-permute-start.13 = (f32[128,512]{1,0:T(8,128)S(1)}, f32[128,512]{1,0:T(8,128)S(1)}, u32[]{:S(2)}, u32[]{:S(2)}) collective-permute-start(f32[128,512]{1,0:T(8,128)S(1)} %collective-permute-done.8.refs_4_), channel_id=1, source_target_pairs={{0,1},{1,0},{2,3},{3,2},{4,5},{5,4},{6,7},{7,6},{8,9},{9,8},{10,11... | collective-permute-start | bytes 786440 | tf_op jit(solution)/shard_map/ppermute | solution.py:231
  51.0 16.8 %all-to-all-start.1 = ((f32[32,8,128]{2,1,0:T(8,128)}), f32[32,8,128]{2,1,0:T(8,128)S(1)}, u32[]{:S(2)}, u32[]{:S(2)}) async-start(f32[32,8,128]{2,1,0:T(8,128)} %bitcast.7), calls=%async_computation.1 | async-start | bytes 262144 | tf_op jit(solution)/shard_map/all_to_all | solution.py:235
  58.4 9.9 %collective-permute-start.12 = (f32[128,512]{1,0:T(8,128)S(1)}, f32[128,512]{1,0:T(8,128)S(1)}, u32[]{:S(2)}, u32[]{:S(2)}) collective-permute-start(f32[128,512]{1,0:T(8,128)S(1)} %collective-permute-done.7.refs_3_), channel_id=1, source_target_pairs={{0,1},{1,0},{2,3},{3,2},{4,5},{5,4},{6,7},{7,6},{8,9},{9,8},{10,11... | collective-permute-start | bytes 786440 | tf_op jit(solution)/shard_map/ppermute | solution.py:231
  58.8 9.9 %collective-permute-start.11 = (f32[128,512]{1,0:T(8,128)S(1)}, f32[128,512]{1,0:T(8,128)S(1)}, u32[]{:S(2)}, u32[]{:S(2)}) collective-permute-start(f32[128,512]{1,0:T(8,128)S(1)} %collective-permute-done.3.refs_2_), channel_id=1, source_target_pairs={{0,1},{1,0},{2,3},{3,2},{4,5},{5,4},{6,7},{7,6},{8,9},{9,8},{10,11... | collective-permute-start | bytes 786440 | tf_op jit(solution)/shard_map/ppermute | solution.py:231
  59.0 9.9 %collective-permute-start.10 = (f32[128,512]{1,0:T(8,128)S(1)}, f32[128,512]{1,0:T(8,128)S(1)}, u32[]{:S(2)}, u32[]{:S(2)}) collective-permute-start(f32[128,512]{1,0:T(8,128)S(1)} %collective-permute-done.1.refs_1_), channel_id=1, source_target_pairs={{0,1},{1,0},{2,3},{3,2},{4,5},{5,4},{6,7},{7,6},{8,9},{9,8},{10,11... | collective-permute-start | bytes 786440 | tf_op jit(solution)/shard_map/ppermute | solution.py:231
  73.5 8.0 %collective-permute-start.18 = (f32[13,8,256]{2,1,0:T(8,128)S(1)}, f32[13,8,256]{2,1,0:T(8,128)S(1)}, u32[]{:S(2)}, u32[]{:S(2)}) collective-permute-start(f32[13,8,256]{2,1,0:T(8,128)S(1)} %get-tuple-element.41), channel_id=1, source_target_pairs={{0,6},{1,7},{2,4},{3,5},{4,2},{5,3},{6,0},{7,1},{8,14},{9,15},{10,... | collective-permute-start | bytes 319496 | tf_op jit(solution)/shard_map/ppermute | solution.py:257
  76.4 5.2 %collective-permute-start.19 = (f32[8,256]{1,0:T(8,128)S(1)}, f32[8,256]{1,0:T(8,128)S(1)}, u32[]{:S(2)}, u32[]{:S(2)}) collective-permute-start(f32[8,256]{1,0:T(8,128)S(1)} %get-tuple-element.42), channel_id=1, source_target_pairs={{0,4},{1,5},{2,6},{3,7},{4,0},{5,1},{6,2},{7,3},{8,12},{9,13},{10,... | collective-permute-start | bytes 24584 | tf_op jit(solution)/shard_map/ppermute | solution.py:256
  82.6 22.9 %collective-permute-start.20 = (f32[11,8,256]{2,1,0:T(8,128)S(1)}, f32[11,8,256]{2,1,0:T(8,128)S(1)}, u32[]{:S(2)}, u32[]{:S(2)}) collective-permute-start(f32[11,8,256]{2,1,0:T(8,128)S(1)} %get-tuple-element.43), channel_id=1, source_target_pairs={{0,8},{1,9},{2,10},{3,11},{4,12},{5,13},{6,14},{7,15},{8,0},{9,1},... | collective-permute-start | bytes 270344 | tf_op jit(solution)/shard_map/ppermute | solution.py:257
  106.5 6.6 %collective-permute-start.22 = (f32[9,8,256]{2,1,0:T(8,128)S(1)}, f32[9,8,256]{2,1,0:T(8,128)S(1)}, u32[]{:S(2)}, u32[]{:S(2)}) collective-permute-start(f32[9,8,256]{2,1,0:T(8,128)S(1)} %get-tuple-element.46), channel_id=1, source_target_pairs={{0,6},{1,7},{2,4},{3,5},{4,2},{5,3},{6,0},{7,1},{8,14},{9,15},{10,... | collective-permute-start | bytes 221192 | tf_op jit(solution)/shard_map/ppermute | solution.py:257
  107.9 5.2 %collective-permute-start.23 = (f32[8,256]{1,0:T(8,128)S(1)}, f32[8,256]{1,0:T(8,128)S(1)}, u32[]{:S(2)}, u32[]{:S(2)}) collective-permute-start(f32[8,256]{1,0:T(8,128)S(1)} %get-tuple-element.47), channel_id=1, source_target_pairs={{0,4},{1,5},{2,6},{3,7},{4,0},{5,1},{6,2},{7,3},{8,12},{9,13},{10,... | collective-permute-start | bytes 24584 | tf_op jit(solution)/shard_map/ppermute | solution.py:256
  113.9 6.0 %collective-permute-start.24 = (f32[7,8,256]{2,1,0:T(8,128)S(1)}, f32[7,8,256]{2,1,0:T(8,128)S(1)}, u32[]{:S(2)}, u32[]{:S(2)}) collective-permute-start(f32[7,8,256]{2,1,0:T(8,128)S(1)} %get-tuple-element.49), channel_id=1, source_target_pairs={{0,24},{1,25},{2,26},{3,27},{4,28},{5,29},{6,30},{7,31},{8,16},{9,... | collective-permute-start | bytes 172040 | tf_op jit(solution)/shard_map/ppermute | solution.py:257
  120.7 6.2 %collective-permute-start.26 = (f32[5,8,256]{2,1,0:T(8,128)S(1)}, f32[5,8,256]{2,1,0:T(8,128)S(1)}, u32[]{:S(2)}, u32[]{:S(2)}) collective-permute-start(f32[5,8,256]{2,1,0:T(8,128)S(1)} %get-tuple-element.52), channel_id=1, source_target_pairs={{0,6},{1,7},{2,4},{3,5},{4,2},{5,3},{6,0},{7,1},{8,14},{9,15},{10,... | collective-permute-start | bytes 122888 | tf_op jit(solution)/shard_map/ppermute | solution.py:257
  127.7 8.4 %collective-permute-start.29 = (f32[3,8,256]{2,1,0:T(8,128)S(1)}, f32[3,8,256]{2,1,0:T(8,128)S(1)}, u32[]{:S(2)}, u32[]{:S(2)}) collective-permute-start(f32[3,8,256]{2,1,0:T(8,128)S(1)} %get-tuple-element.56), channel_id=1, source_target_pairs={{0,8},{1,9},{2,10},{3,11},{4,12},{5,13},{6,14},{7,15},{8,0},{9,1},... | collective-permute-start | bytes 73736 | tf_op jit(solution)/shard_map/ppermute | solution.py:257
  138.6 5.7 %collective-permute-start.28 = (f32[8,256]{1,0:T(8,128)S(1)}, f32[8,256]{1,0:T(8,128)S(1)}, u32[]{:S(2)}, u32[]{:S(2)}) collective-permute-start(f32[8,256]{1,0:T(8,128)S(1)} %get-tuple-element.55.final_ref), channel_id=1, source_target_pairs={{0,6},{1,7},{2,4},{3,5},{4,2},{5,3},{6,0},{7,1},{16,22},{17,23},{1... | collective-permute-start | bytes 24584 | tf_op jit(solution)/shard_map/ppermute | solution.py:202
  (14 other events, 62.9 us)

commit v2 on v1

--- a/solution.py
+++ b/solution.py
@@ -29,6 +29,10 @@
     mid = rest.astype(jnp.bfloat16)
     lo = (rest - mid.astype(jnp.float32)).astype(jnp.bfloat16)
     return hi, mid, lo
+
+
+def turned_quad(quad):
+    return 1 - ((quad >> 1) & 1)
 
 
 def take_kernel(first_ref, pivots_ref, rhs_ref, out_ref):
@@ -40,14 +44,15 @@
     got = jnp.dot(parts, pick, preferred_element_type=jnp.float32)
     got = (got[2 * count :] + got[count : 2 * count]) + got[:count]
     pieces, _, length = out_ref.shape
+    shift = 2 * turned_quad(pl.program_id(0))
     for n in range(pieces):
-        out_ref[n] = got[:, n * length : (n + 1) * length]
+        out_ref[lax.rem(n + shift, pieces)] = got[:, n * length : (n + 1) * length]
 
 
 def take_columns(rhs, pivots, first, piece_len):
     count, source = rhs.shape
     total = pivots.shape[0]
-    step = source
+    step = QUAD * piece_len
     return pl.pallas_call(
         take_kernel,
         grid=(total // step,),
@@ -56,7 +61,9 @@
             pl.BlockSpec((1, step), lambda n: (0, n)),
             pl.BlockSpec((count, source), lambda n: (0, 0)),
         ],
-        out_specs=pl.BlockSpec((step // piece_len, count, piece_len), lambda n: (n, 0, 0)),
+        out_specs=pl.BlockSpec(
+            (step // piece_len, count, piece_len), lambda n: (n ^ turned_quad(n), 0, 0)
+        ),
         out_shape=jax.ShapeDtypeStruct((total // piece_len, count, piece_len), jnp.float32),
         compiler_params=pltpu.CompilerParams(vmem_limit_bytes=VMEM_LIMIT),
     )(first.reshape(1), pivots.reshape(1, total), rhs)
@@ -202,10 +209,7 @@
         return jnp.where(turned, lax.ppermute(shard, ("quad", "i"), there), shard)
 
     lower = mirror(factor.reshape(block_len, piece_len))
-    order = pivots.reshape(quads // 2, 4, -1)
-    even = lax.broadcasted_iota(jnp.int32, order.shape, 0) % 2 == 0
-    order = jnp.where(even, order[:, ::-1], order).reshape(-1)
-    taken = take_columns(rhs, order, flat * source_len, piece_len)
+    taken = take_columns(rhs, pivots, flat * source_len, piece_len)
     inverse = diag_inv[0]
     scaled = dot(lower, inverse, ((0,), (1,)))
     own_rows = lax.dynamic_slice_in_dim(inverse, at_i * piece_len, piece_len, 0)

time: 156 us -> 156 us (level)
  no operation moved by 1% of the time
where the time goes in v2:
time: 156 us; the launch traced here: 155 us
  starting transfers between devices  69.5 us (45%)
  waiting for transfers between devices  57.2 us (37%)
  Pallas kernels  12.8 us (8%)
  blocking collectives  10.6 us (7%)
  local copies, waits for them, and re-layouts  3.68 us (2%)
    ppermute x7, starting transfers between devices, solve(): got = lax.ppermute(sent, ('quad', 'i'), near_to)  30.9 us
    ppermute x7, waiting for transfers between devices, solve(): far = lax.ppermute(same, ('quad', 'i'), far_to)  27.8 us
    ppermute x8, waiting for transfers between devices, shift(): lax.ppermute(shard, 'row', [(r, (r + by) % rows) for r in range(rows)])  17.1 us
    ppermute x8, starting transfers between devices, shift(): lax.ppermute(shard, 'row', [(r, (r + by) % rows) for r in range(rows)])  16.9 us
    all_to_all x1, blocking collectives, solve(): lax.all_to_all(jnp.broadcast_to(final[None], (rows, group, piece_len)), '...  10.6 us
    all_to_all x1, waiting for transfers between devices, solve(): incoming = lax.all_to_all(outgoing, ('row', 'i'), 0, 0, tiled=True)  8.55 us
    all_to_all x1, starting transfers between devices, solve(): spread = lax.all_to_all(taken, ('quad', 'i'), 0, 0, tiled=True)  7.62 us
    all_to_all x1, starting transfers between devices, solve(): incoming = lax.all_to_all(outgoing, ('row', 'i'), 0, 0, tiled=True)  7.34 us
  transfers between devices with their start and end apart: 35, of which 14 were waited for; matrix products, arithmetic and copies ran while one was open for 2% of the time, Pallas kernels for 0%

profile of v2, /device:TPU:2, one launch (start us, length us, event | category | flops | bytes accessed | tf_op | source)
XLA Modules:
  0.0 155.4 jit_solution(14389146622949818263)
XLA Ops:
  1.6 4.0 %shard_map.46 = f32[32,64,128]{2,1,0:T(8,128)} custom-call(s32[1]{0:T(128)} %bitcast.5.first_ref, s32[1,4096]{1,0:T(1,128)S(1)} %bitcast.18, f32[64,512]{1,0:T(8,128)S(1)} %copy-done), custom_call_target="tpu_custom_call" | custom-call | tf_op jit(solution)/shard_map/pallas_call | solution.py:56
  5.7 7.6 %all-to-all-start = ((f32[32,64,128]{2,1,0:T(8,128)}), f32[32,64,128]{2,1,0:T(8,128)S(1)}, u32[]{:S(2)}, u32[]{:S(2)}) async-start(f32[32,64,128]{2,1,0:T(8,128)} %shard_map.46), calls=%async_computation | async-start | bytes 2097152 | tf_op jit(solution)/shard_map/all_to_all | solution.py:224
  15.3 6.4 %collective-permute-start.3 = (f32[128,512]{1,0:T(8,128)S(1)}, f32[128,512]{1,0:T(8,128)S(1)}, u32[]{:S(2)}, u32[]{:S(2)}) collective-permute-start(f32[128,512]{1,0:T(8,128)S(1)} %fusion.refs_0_), channel_id=1, source_target_pairs={{0,192},{32,224},{64,0},{96,32},{128,64},{160,96},{192,128},{224,1... | collective-permute-start | bytes 786440 | tf_op jit(solution)/shard_map/ppermute | solution.py:219
  21.7 3.7 %collective-permute-start.8 = (f32[128,512]{1,0:T(8,128)S(1)}, f32[128,512]{1,0:T(8,128)S(1)}, u32[]{:S(2)}, u32[]{:S(2)}) collective-permute-start(f32[128,512]{1,0:T(8,128)S(1)} %fusion.refs_0_), channel_id=1, source_target_pairs={{0,224},{32,0},{64,32},{96,64},{128,96},{160,128},{192,160},{224,1... | collective-permute-start | bytes 786440 | tf_op jit(solution)/shard_map/ppermute | solution.py:219
  25.4 8.2 %collective-permute-done.3.refs_2_ = f32[128,512]{1,0:T(8,128)S(1)} collective-permute-done((f32[128,512]{1,0:T(8,128)S(1)}, f32[128,512]{1,0:T(8,128)S(1)}, u32[]{:S(2)}, u32[]{:S(2)}) %collective-permute-start.3) | collective-permute-done | bytes 262176 | tf_op jit(solution)/shard_map/ppermute | solution.py:219
  33.6 2.7 %collective-permute-start.6 = (f32[128,512]{1,0:T(8,128)S(1)}, f32[128,512]{1,0:T(8,128)S(1)}, u32[]{:S(2)}, u32[]{:S(2)}) collective-permute-start(f32[128,512]{1,0:T(8,128)S(1)} %collective-permute-done.3.refs_2_), channel_id=1, source_target_pairs={{0,224},{32,0},{64,32},{96,64},{128,96},{160,128},{192,160},{224,1... | collective-permute-start | bytes 786440 | tf_op jit(solution)/shard_map/ppermute | solution.py:219
  36.3 2.1 %collective-permute-start.4 = (f32[64,512]{1,0:T(8,128)S(1)}, f32[64,512]{1,0:T(8,128)}, u32[]{:S(2)}, u32[]{:S(2)}) collective-permute-start(f32[64,512]{1,0:T(8,128)S(1)} %slice.17), channel_id=1, source_target_pairs={{0,192},{32,224},{64,0},{96,32},{128,64},{160,96},{192,128},{224,1... | collective-permute-start | bytes 393224 | tf_op jit(solution)/shard_map/ppermute | solution.py:219
  38.4 2.0 %collective-permute-start.5 = (f32[128,512]{1,0:T(8,128)S(1)}, f32[128,512]{1,0:T(8,128)S(1)}, u32[]{:S(2)}, u32[]{:S(2)}) collective-permute-start(f32[128,512]{1,0:T(8,128)S(1)} %collective-permute-done.1.refs_1_), channel_id=1, source_target_pairs={{0,32},{32,64},{64,96},{96,128},{128,160},{160,192},{192,224},{224... | collective-permute-start | bytes 786440 | tf_op jit(solution)/shard_map/ppermute | solution.py:219
  41.1 2.1 %collective-permute-done.7.refs_3_ = f32[128,512]{1,0:T(8,128)S(1)} collective-permute-done((f32[128,512]{1,0:T(8,128)S(1)}, f32[128,512]{1,0:T(8,128)S(1)}, u32[]{:S(2)}, u32[]{:S(2)}) %collective-permute-start.7) | collective-permute-done | bytes 262176 | tf_op jit(solution)/shard_map/ppermute | solution.py:219
  43.2 6.9 %collective-permute-done.4.refs_6_ = f32[64,512]{1,0:T(8,128)} collective-permute-done((f32[64,512]{1,0:T(8,128)S(1)}, f32[64,512]{1,0:T(8,128)}, u32[]{:S(2)}, u32[]{:S(2)}) %collective-permute-start.4) | collective-permute-done | bytes 131104 | tf_op jit(solution)/shard_map/ppermute | solution.py:219
  50.8 7.3 %all-to-all-start.1 = ((f32[32,8,128]{2,1,0:T(8,128)}), f32[32,8,128]{2,1,0:T(8,128)S(1)}, u32[]{:S(2)}, u32[]{:S(2)}) async-start(f32[32,8,128]{2,1,0:T(8,128)} %bitcast.8), calls=%async_computation.1 | async-start | bytes 262144 | tf_op jit(solution)/shard_map/all_to_all | solution.py:239
  59.0 8.5 %all-to-all-done.1 = f32[32,8,128]{2,1,0:T(8,128)S(1)} async-done(((f32[32,8,128]{2,1,0:T(8,128)}), f32[32,8,128]{2,1,0:T(8,128)S(1)}, u32[]{:S(2)}, u32[]{:S(2)}) %all-to-all-start.1) | async-done | bytes 131104 | tf_op jit(solution)/shard_map/all_to_all | solution.py:239
  73.3 2.9 %collective-permute-start.18 = (f32[13,8,256]{2,1,0:T(8,128)S(1)}, f32[13,8,256]{2,1,0:T(8,128)S(1)}, u32[]{:S(2)}, u32[]{:S(2)}) collective-permute-start(f32[13,8,256]{2,1,0:T(8,128)S(1)} %get-tuple-element.41), channel_id=1, source_target_pairs={{0,6},{1,7},{2,4},{3,5},{4,2},{5,3},{6,0},{7,1},{8,14},{9,15},{10,... | collective-permute-start | bytes 319496 | tf_op jit(solution)/shard_map/ppermute | solution.py:261
  77.0 4.3 %collective-permute-done.19.far_ref = f32[8,256]{1,0:T(8,128)S(1)} collective-permute-done((f32[8,256]{1,0:T(8,128)S(1)}, f32[8,256]{1,0:T(8,128)S(1)}, u32[]{:S(2)}, u32[]{:S(2)}) %collective-permute-start.19) | collective-permute-done | bytes 8224 | tf_op jit(solution)/shard_map/ppermute | solution.py:260
  82.3 18.4 %collective-permute-start.20 = (f32[11,8,256]{2,1,0:T(8,128)S(1)}, f32[11,8,256]{2,1,0:T(8,128)S(1)}, u32[]{:S(2)}, u32[]{:S(2)}) collective-permute-start(f32[11,8,256]{2,1,0:T(8,128)S(1)} %get-tuple-element.43), channel_id=1, source_target_pairs={{0,8},{1,9},{2,10},{3,11},{4,12},{5,13},{6,14},{7,15},{8,0},{9,1},... | collective-permute-start | bytes 270344 | tf_op jit(solution)/shard_map/ppermute | solution.py:261
  100.7 4.5 %collective-permute-done.21.far_ref = f32[8,256]{1,0:T(8,128)S(1)} collective-permute-done((f32[8,256]{1,0:T(8,128)S(1)}, f32[8,256]{1,0:T(8,128)S(1)}, u32[]{:S(2)}, u32[]{:S(2)}) %collective-permute-start.21) | collective-permute-done | bytes 8224 | tf_op jit(solution)/shard_map/ppermute | solution.py:260
  108.2 4.6 %collective-permute-done.23.far_ref = f32[8,256]{1,0:T(8,128)S(1)} collective-permute-done((f32[8,256]{1,0:T(8,128)S(1)}, f32[8,256]{1,0:T(8,128)S(1)}, u32[]{:S(2)}, u32[]{:S(2)}) %collective-permute-start.23) | collective-permute-done | bytes 8224 | tf_op jit(solution)/shard_map/ppermute | solution.py:260
  115.6 4.0 %collective-permute-done.25.far_ref = f32[8,256]{1,0:T(8,128)S(1)} collective-permute-done((f32[8,256]{1,0:T(8,128)S(1)}, f32[8,256]{1,0:T(8,128)S(1)}, u32[]{:S(2)}, u32[]{:S(2)}) %collective-permute-start.25) | collective-permute-done | bytes 8224 | tf_op jit(solution)/shard_map/ppermute | solution.py:260
  123.0 3.7 %collective-permute-done.27.far_ref = f32[8,256]{1,0:T(8,128)S(1)} collective-permute-done((f32[8,256]{1,0:T(8,128)S(1)}, f32[8,256]{1,0:T(8,128)S(1)}, u32[]{:S(2)}, u32[]{:S(2)}) %collective-permute-start.27) | collective-permute-done | bytes 8224 | tf_op jit(solution)/shard_map/ppermute | solution.py:260
  127.4 3.8 %collective-permute-start.29 = (f32[3,8,256]{2,1,0:T(8,128)S(1)}, f32[3,8,256]{2,1,0:T(8,128)S(1)}, u32[]{:S(2)}, u32[]{:S(2)}) collective-permute-start(f32[3,8,256]{2,1,0:T(8,128)S(1)} %get-tuple-element.56), channel_id=1, source_target_pairs={{0,8},{1,9},{2,10},{3,11},{4,12},{5,13},{6,14},{7,15},{8,0},{9,1},... | collective-permute-start | bytes 73736 | tf_op jit(solution)/shard_map/ppermute | solution.py:261
  131.3 4.5 %collective-permute-done.30.far_ref = f32[8,256]{1,0:T(8,128)S(1)} collective-permute-done((f32[8,256]{1,0:T(8,128)S(1)}, f32[8,256]{1,0:T(8,128)S(1)}, u32[]{:S(2)}, u32[]{:S(2)}) %collective-permute-start.30) | collective-permute-done | bytes 8224 | tf_op jit(solution)/shard_map/ppermute | solution.py:260
  139.1 2.3 %collective-permute-done.31.near_ref = f32[1,8,256]{2,1,0:T(8,128)S(1)} collective-permute-done((f32[1,8,256]{2,1,0:T(8,128)S(1)}, f32[1,8,256]{2,1,0:T(8,128)S(1)}, u32[]{:S(2)}, u32[]{:S(2)}) %collective-permute-start.31) | collective-permute-done | bytes 8224 | tf_op jit(solution)/shard_map/ppermute | solution.py:261
  141.4 2.1 %collective-permute-done.32.far_ref = f32[8,256]{1,0:T(8,128)S(1)} collective-permute-done((f32[8,256]{1,0:T(8,128)S(1)}, f32[8,256]{1,0:T(8,128)S(1)}, u32[]{:S(2)}, u32[]{:S(2)}) %collective-permute-start.32) | collective-permute-done | bytes 8224 | tf_op jit(solution)/shard_map/ppermute | solution.py:260
  144.1 10.6 %all_to_all.15 = f32[8,8,128]{2,1,0:T(8,128)S(1)} all-to-all(f32[8,8,128]{2,1,0:T(8,128)S(1)} %broadcast_in_dim.15), channel_id=1, replica_groups=mesh['row'=8,'quad'=8,'i'=4] {'row'}, dimensions={0} | all-to-all | bytes 65536 | tf_op jit(solution)/shard_map/all_to_all | solution.py:272
  (75 shorter events, 27.7 us)
Async XLA Ops:
  5.7 44.4 %all-to-all-start = ((f32[32,64,128]{2,1,0:T(8,128)}), f32[32,64,128]{2,1,0:T(8,128)S(1)}, u32[]{:S(2)}, u32[]{:S(2)}) async-start(f32[32,64,128]{2,1,0:T(8,128)} %shard_map.46), calls=%async_computation | async-start | bytes 2097152 | tf_op jit(solution)/shard_map/all_to_all | solution.py:224
  15.3 18.2 %collective-permute-start.3 = (f32[128,512]{1,0:T(8,128)S(1)}, f32[128,512]{1,0:T(8,128)S(1)}, u32[]{:S(2)}, u32[]{:S(2)}) collective-permute-start(f32[128,512]{1,0:T(8,128)S(1)} %fusion.refs_0_), channel_id=1, source_target_pairs={{0,192},{32,224},{64,0},{96,32},{128,64},{160,96},{192,128},{224,1... | collective-permute-start | bytes 786440 | tf_op jit(solution)/shard_map/ppermute | solution.py:219
  21.7 16.7 %collective-permute-start.1 = (f32[128,512]{1,0:T(8,128)S(1)}, f32[128,512]{1,0:T(8,128)S(1)}, u32[]{:S(2)}, u32[]{:S(2)}) collective-permute-start(f32[128,512]{1,0:T(8,128)S(1)} %fusion.refs_0_), channel_id=1, source_target_pairs={{0,64},{32,96},{64,128},{96,160},{128,192},{160,224},{192,0},{224,... | collective-permute-start | bytes 786440 | tf_op jit(solution)/shard_map/ppermute | solution.py:219
  21.7 19.4 %collective-permute-start.8 = (f32[128,512]{1,0:T(8,128)S(1)}, f32[128,512]{1,0:T(8,128)S(1)}, u32[]{:S(2)}, u32[]{:S(2)}) collective-permute-start(f32[128,512]{1,0:T(8,128)S(1)} %fusion.refs_0_), channel_id=1, source_target_pairs={{0,224},{32,0},{64,32},{96,64},{128,96},{160,128},{192,160},{224,1... | collective-permute-start | bytes 786440 | tf_op jit(solution)/shard_map/ppermute | solution.py:219
  25.4 17.8 %collective-permute-start.7 = (f32[128,512]{1,0:T(8,128)S(1)}, f32[128,512]{1,0:T(8,128)S(1)}, u32[]{:S(2)}, u32[]{:S(2)}) collective-permute-start(f32[128,512]{1,0:T(8,128)S(1)} %fusion.refs_0_), channel_id=1, source_target_pairs={{0,32},{32,64},{64,96},{96,128},{128,160},{160,192},{192,224},{224... | collective-permute-start | bytes 786440 | tf_op jit(solution)/shard_map/ppermute | solution.py:219
  33.6 24.9 %collective-permute-start.6 = (f32[128,512]{1,0:T(8,128)S(1)}, f32[128,512]{1,0:T(8,128)S(1)}, u32[]{:S(2)}, u32[]{:S(2)}) collective-permute-start(f32[128,512]{1,0:T(8,128)S(1)} %collective-permute-done.3.refs_2_), channel_id=1, source_target_pairs={{0,224},{32,0},{64,32},{96,64},{128,96},{160,128},{192,160},{224,1... | collective-permute-start | bytes 786440 | tf_op jit(solution)/shard_map/ppermute | solution.py:219
  36.3 13.8 %collective-permute-start.4 = (f32[64,512]{1,0:T(8,128)S(1)}, f32[64,512]{1,0:T(8,128)}, u32[]{:S(2)}, u32[]{:S(2)}) collective-permute-start(f32[64,512]{1,0:T(8,128)S(1)} %slice.17), channel_id=1, source_target_pairs={{0,192},{32,224},{64,0},{96,32},{128,64},{160,96},{192,128},{224,1... | collective-permute-start | bytes 393224 | tf_op jit(solution)/shard_map/ppermute | solution.py:219
  38.4 20.3 %collective-permute-start.5 = (f32[128,512]{1,0:T(8,128)S(1)}, f32[128,512]{1,0:T(8,128)S(1)}, u32[]{:S(2)}, u32[]{:S(2)}) collective-permute-start(f32[128,512]{1,0:T(8,128)S(1)} %collective-permute-done.1.refs_1_), channel_id=1, source_target_pairs={{0,32},{32,64},{64,96},{96,128},{128,160},{160,192},{192,224},{224... | collective-permute-start | bytes 786440 | tf_op jit(solution)/shard_map/ppermute | solution.py:219
  41.1 17.0 %collective-permute-start.2 = (f32[64,512]{1,0:T(8,128)}, f32[64,512]{1,0:T(8,128)}, u32[]{:S(2)}, u32[]{:S(2)}) collective-permute-start(f32[64,512]{1,0:T(8,128)} %slice.16), channel_id=1, source_target_pairs={{0,64},{32,96},{64,128},{96,160},{128,192},{160,224},{192,0},{224,... | collective-permute-start | bytes 393224 | tf_op jit(solution)/shard_map/ppermute | solution.py:219
  43.2 24.4 %collective-permute-start.9 = (f32[128,512]{1,0:T(8,128)S(1)}, f32[128,512]{1,0:T(8,128)S(1)}, u32[]{:S(2)}, u32[]{:S(2)}) collective-permute-start(f32[128,512]{1,0:T(8,128)S(1)} %fusion.refs_0_), channel_id=1, source_target_pairs={{0,1},{1,0},{2,3},{3,2},{4,5},{5,4},{6,7},{7,6},{8,9},{9,8},{10,11... | collective-permute-start | bytes 786440 | tf_op jit(solution)/shard_map/ppermute | solution.py:235
  50.1 17.6 %collective-permute-start.13 = (f32[128,512]{1,0:T(8,128)S(1)}, f32[128,512]{1,0:T(8,128)S(1)}, u32[]{:S(2)}, u32[]{:S(2)}) collective-permute-start(f32[128,512]{1,0:T(8,128)S(1)} %collective-permute-done.8.refs_4_), channel_id=1, source_target_pairs={{0,1},{1,0},{2,3},{3,2},{4,5},{5,4},{6,7},{7,6},{8,9},{9,8},{10,11... | collective-permute-start | bytes 786440 | tf_op jit(solution)/shard_map/ppermute | solution.py:235
  50.8 16.8 %all-to-all-start.1 = ((f32[32,8,128]{2,1,0:T(8,128)}), f32[32,8,128]{2,1,0:T(8,128)S(1)}, u32[]{:S(2)}, u32[]{:S(2)}) async-start(f32[32,8,128]{2,1,0:T(8,128)} %bitcast.8), calls=%async_computation.1 | async-start | bytes 262144 | tf_op jit(solution)/shard_map/all_to_all | solution.py:239
  58.1 9.9 %collective-permute-start.12 = (f32[128,512]{1,0:T(8,128)S(1)}, f32[128,512]{1,0:T(8,128)S(1)}, u32[]{:S(2)}, u32[]{:S(2)}) collective-permute-start(f32[128,512]{1,0:T(8,128)S(1)} %collective-permute-done.7.refs_3_), channel_id=1, source_target_pairs={{0,1},{1,0},{2,3},{3,2},{4,5},{5,4},{6,7},{7,6},{8,9},{9,8},{10,11... | collective-permute-start | bytes 786440 | tf_op jit(solution)/shard_map/ppermute | solution.py:235
  58.5 9.9 %collective-permute-start.11 = (f32[128,512]{1,0:T(8,128)S(1)}, f32[128,512]{1,0:T(8,128)S(1)}, u32[]{:S(2)}, u32[]{:S(2)}) collective-permute-start(f32[128,512]{1,0:T(8,128)S(1)} %collective-permute-done.3.refs_2_), channel_id=1, source_target_pairs={{0,1},{1,0},{2,3},{3,2},{4,5},{5,4},{6,7},{7,6},{8,9},{9,8},{10,11... | collective-permute-start | bytes 786440 | tf_op jit(solution)/shard_map/ppermute | solution.py:235
  58.7 9.9 %collective-permute-start.10 = (f32[128,512]{1,0:T(8,128)S(1)}, f32[128,512]{1,0:T(8,128)S(1)}, u32[]{:S(2)}, u32[]{:S(2)}) collective-permute-start(f32[128,512]{1,0:T(8,128)S(1)} %collective-permute-done.1.refs_1_), channel_id=1, source_target_pairs={{0,1},{1,0},{2,3},{3,2},{4,5},{5,4},{6,7},{7,6},{8,9},{9,8},{10,11... | collective-permute-start | bytes 786440 | tf_op jit(solution)/shard_map/ppermute | solution.py:235
  73.3 8.0 %collective-permute-start.18 = (f32[13,8,256]{2,1,0:T(8,128)S(1)}, f32[13,8,256]{2,1,0:T(8,128)S(1)}, u32[]{:S(2)}, u32[]{:S(2)}) collective-permute-start(f32[13,8,256]{2,1,0:T(8,128)S(1)} %get-tuple-element.41), channel_id=1, source_target_pairs={{0,6},{1,7},{2,4},{3,5},{4,2},{5,3},{6,0},{7,1},{8,14},{9,15},{10,... | collective-permute-start | bytes 319496 | tf_op jit(solution)/shard_map/ppermute | solution.py:261
  76.1 5.2 %collective-permute-start.19 = (f32[8,256]{1,0:T(8,128)S(1)}, f32[8,256]{1,0:T(8,128)S(1)}, u32[]{:S(2)}, u32[]{:S(2)}) collective-permute-start(f32[8,256]{1,0:T(8,128)S(1)} %get-tuple-element.42), channel_id=1, source_target_pairs={{0,4},{1,5},{2,6},{3,7},{4,0},{5,1},{6,2},{7,3},{8,12},{9,13},{10,... | collective-permute-start | bytes 24584 | tf_op jit(solution)/shard_map/ppermute | solution.py:260
  82.3 22.9 %collective-permute-start.20 = (f32[11,8,256]{2,1,0:T(8,128)S(1)}, f32[11,8,256]{2,1,0:T(8,128)S(1)}, u32[]{:S(2)}, u32[]{:S(2)}) collective-permute-start(f32[11,8,256]{2,1,0:T(8,128)S(1)} %get-tuple-element.43), channel_id=1, source_target_pairs={{0,8},{1,9},{2,10},{3,11},{4,12},{5,13},{6,14},{7,15},{8,0},{9,1},... | collective-permute-start | bytes 270344 | tf_op jit(solution)/shard_map/ppermute | solution.py:261
  106.2 6.6 %collective-permute-start.22 = (f32[9,8,256]{2,1,0:T(8,128)S(1)}, f32[9,8,256]{2,1,0:T(8,128)S(1)}, u32[]{:S(2)}, u32[]{:S(2)}) collective-permute-start(f32[9,8,256]{2,1,0:T(8,128)S(1)} %get-tuple-element.46), channel_id=1, source_target_pairs={{0,6},{1,7},{2,4},{3,5},{4,2},{5,3},{6,0},{7,1},{8,14},{9,15},{10,... | collective-permute-start | bytes 221192 | tf_op jit(solution)/shard_map/ppermute | solution.py:261
  113.7 6.0 %collective-permute-start.24 = (f32[7,8,256]{2,1,0:T(8,128)S(1)}, f32[7,8,256]{2,1,0:T(8,128)S(1)}, u32[]{:S(2)}, u32[]{:S(2)}) collective-permute-start(f32[7,8,256]{2,1,0:T(8,128)S(1)} %get-tuple-element.49), channel_id=1, source_target_pairs={{0,24},{1,25},{2,26},{3,27},{4,28},{5,29},{6,30},{7,31},{8,16},{9,... | collective-permute-start | bytes 172040 | tf_op jit(solution)/shard_map/ppermute | solution.py:261
  120.5 6.2 %collective-permute-start.26 = (f32[5,8,256]{2,1,0:T(8,128)S(1)}, f32[5,8,256]{2,1,0:T(8,128)S(1)}, u32[]{:S(2)}, u32[]{:S(2)}) collective-permute-start(f32[5,8,256]{2,1,0:T(8,128)S(1)} %get-tuple-element.52), channel_id=1, source_target_pairs={{0,6},{1,7},{2,4},{3,5},{4,2},{5,3},{6,0},{7,1},{8,14},{9,15},{10,... | collective-permute-start | bytes 122888 | tf_op jit(solution)/shard_map/ppermute | solution.py:261
  127.4 8.4 %collective-permute-start.29 = (f32[3,8,256]{2,1,0:T(8,128)S(1)}, f32[3,8,256]{2,1,0:T(8,128)S(1)}, u32[]{:S(2)}, u32[]{:S(2)}) collective-permute-start(f32[3,8,256]{2,1,0:T(8,128)S(1)} %get-tuple-element.56), channel_id=1, source_target_pairs={{0,8},{1,9},{2,10},{3,11},{4,12},{5,13},{6,14},{7,15},{8,0},{9,1},... | collective-permute-start | bytes 73736 | tf_op jit(solution)/shard_map/ppermute | solution.py:261
  138.4 5.2 %collective-permute-start.32 = (f32[8,256]{1,0:T(8,128)S(1)}, f32[8,256]{1,0:T(8,128)S(1)}, u32[]{:S(2)}, u32[]{:S(2)}) collective-permute-start(f32[8,256]{1,0:T(8,128)S(1)} %get-tuple-element.59), channel_id=1, source_target_pairs={{0,4},{1,5},{2,6},{3,7},{4,0},{5,1},{6,2},{7,3},{8,12},{9,13},{10,... | collective-permute-start | bytes 24584 | tf_op jit(solution)/shard_map/ppermute | solution.py:260
  138.4 5.7 %collective-permute-start.28 = (f32[8,256]{1,0:T(8,128)S(1)}, f32[8,256]{1,0:T(8,128)S(1)}, u32[]{:S(2)}, u32[]{:S(2)}) collective-permute-start(f32[8,256]{1,0:T(8,128)S(1)} %get-tuple-element.55.final_ref), channel_id=1, source_target_pairs={{0,6},{1,7},{2,4},{3,5},{4,2},{5,3},{6,0},{7,1},{16,22},{17,23},{1... | collective-permute-start | bytes 24584 | tf_op jit(solution)/shard_map/ppermute | solution.py:209
  (15 other events, 63.7 us)

commit v3 on v2

--- a/solution.py
+++ b/solution.py
@@ -223,14 +223,8 @@
     first += [shift(slot, 1), shift(slot, -1)]
     spread = lax.all_to_all(taken, ("quad", "i"), 0, 0, tiled=True)
     piece = spread.sum(axis=0)
-    cut = piece_len // 2
-    second = [
-        shift(first[0][:cut], 2),
-        shift(first[1][cut:], -2),
-        shift(first[0], 1),
-        shift(first[1], -1),
-    ]
-    parts = ((0, 0), (-2, 0), (2, 0), (-1, 0), (1, 0), (4, 0), (4, cut), (-3, 0), (3, 0))
+    second = [shift(first[0], 2), shift(first[0], 1), shift(first[1], -1)]
+    parts = ((0, 0), (-2, 0), (2, 0), (-1, 0), (1, 0), (-4, 0), (-3, 0), (3, 0))
     near_rows = [slot, *first]
     theirs = [lax.ppermute(rows_of, "i", partner) for rows_of in near_rows]
     outgoing = jnp.broadcast_to(

time: 156 us -> 137 us (0.88)
  starting transfers between devices: 69.5 us -> 48.8 us
    ppermute x7, starting transfers between devices: 30.9 us -> 12.6 us  [solve(): got = lax.ppermute(sent, ('quad', 'i'), near_to)]
    all_to_all x1, waiting for transfers between devices: 8.55 us -> 3.14 us  [solve(): incoming = lax.all_to_all(outgoing, ('row', 'i'), 0, 0, tiled=True)]
    ppermute x8 -> x7, waiting for transfers between devices: 17.1 us -> 22.3 us  [shift(): lax.ppermute(shard, 'row', [(r, (r + by) % rows) for r in range(rows)])]
    ppermute x8 -> x7, starting transfers between devices: 16.9 us -> 13.8 us  [shift(): lax.ppermute(shard, 'row', [(r, (r + by) % rows) for r in range(rows)])]
    all_to_all x1, starting transfers between devices: 7.62 us -> 9.36 us  [solve(): spread = lax.all_to_all(taken, ('quad', 'i'), 0, 0, tiled=True)]
  transfers between devices with their start and end apart: 35 -> 33, of which waited for: 14 -> 18; matrix products, arithmetic and copies ran while one was open for 2% -> 2% of each run, Pallas kernels for 0% -> 3%
where the time goes in v3:
time: 137 us; the launch traced here: 135 us
  waiting for transfers between devices  56.4 us (41%)
  starting transfers between devices  48.8 us (36%)
  Pallas kernels  12.8 us (9%)
  blocking collectives  11.6 us (8%)
  local copies, waits for them, and re-layouts  2.99 us (2%)
    ppermute x7, waiting for transfers between devices, solve(): far = lax.ppermute(same, ('quad', 'i'), far_to)  26.8 us
    ppermute x7, waiting for transfers between devices, shift(): lax.ppermute(shard, 'row', [(r, (r + by) % rows) for r in range(rows)])  22.3 us
    ppermute x7, starting transfers between devices, shift(): lax.ppermute(shard, 'row', [(r, (r + by) % rows) for r in range(rows)])  13.8 us
    ppermute x7, starting transfers between devices, solve(): got = lax.ppermute(sent, ('quad', 'i'), near_to)  12.6 us
    all_to_all x1, blocking collectives, solve(): lax.all_to_all(jnp.broadcast_to(final[None], (rows, group, piece_len)), '...  11.6 us
    all_to_all x1, starting transfers between devices, solve(): spread = lax.all_to_all(taken, ('quad', 'i'), 0, 0, tiled=True)  9.36 us
    pallas_call x8, Pallas kernels, call(): pl.pallas_call(kernel, in_specs=[pl.BlockSpec(memory_space=pltpu.SMEM)] +...  6.93 us
    all_to_all x1, starting transfers between devices, solve(): incoming = lax.all_to_all(outgoing, ('row', 'i'), 0, 0, tiled=True)  6.35 us
  transfers between devices with their start and end apart: 33, of which 18 were waited for; matrix products, arithmetic and copies ran while one was open for 2% of the time, Pallas kernels for 3%

profile of v3, /device:TPU:2, one launch (start us, length us, event | category | flops | bytes accessed | tf_op | source)
XLA Modules:
  0.0 135.3 jit_solution(12308293070429650408)
XLA Ops:
  2.3 4.1 %shard_map.46 = f32[32,64,128]{2,1,0:T(8,128)} custom-call(s32[1]{0:T(128)} %bitcast.5.first_ref, s32[1,4096]{1,0:T(1,128)S(1)} %bitcast.18, f32[64,512]{1,0:T(8,128)S(1)} %copy-done), custom_call_target="tpu_custom_call" | custom-call | tf_op jit(solution)/shard_map/pallas_call | solution.py:56
  6.4 9.4 %all-to-all-start = ((f32[32,64,128]{2,1,0:T(8,128)}), f32[32,64,128]{2,1,0:T(8,128)}, u32[]{:S(2)}, u32[]{:S(2)}) async-start(f32[32,64,128]{2,1,0:T(8,128)} %shard_map.46), calls=%async_computation | async-start | bytes 2097152 | tf_op jit(solution)/shard_map/all_to_all | solution.py:224
  17.1 6.4 %collective-permute-start.4 = (f32[128,512]{1,0:T(8,128)S(1)}, f32[128,512]{1,0:T(8,128)S(1)}, u32[]{:S(2)}, u32[]{:S(2)}) collective-permute-start(f32[128,512]{1,0:T(8,128)S(1)} %fusion.refs_0_), channel_id=1, source_target_pairs={{0,192},{32,224},{64,0},{96,32},{128,64},{160,96},{192,128},{224,1... | collective-permute-start | bytes 786440 | tf_op jit(solution)/shard_map/ppermute | solution.py:219
  23.4 3.7 %collective-permute-start.7 = (f32[128,512]{1,0:T(8,128)S(1)}, f32[128,512]{1,0:T(8,128)S(1)}, u32[]{:S(2)}, u32[]{:S(2)}) collective-permute-start(f32[128,512]{1,0:T(8,128)S(1)} %fusion.refs_0_), channel_id=1, source_target_pairs={{0,224},{32,0},{64,32},{96,64},{128,96},{160,128},{192,160},{224,1... | collective-permute-start | bytes 786440 | tf_op jit(solution)/shard_map/ppermute | solution.py:219
  27.1 8.2 %collective-permute-done.4.refs_2_ = f32[128,512]{1,0:T(8,128)S(1)} collective-permute-done((f32[128,512]{1,0:T(8,128)S(1)}, f32[128,512]{1,0:T(8,128)S(1)}, u32[]{:S(2)}, u32[]{:S(2)}) %collective-permute-start.4) | collective-permute-done | bytes 262176 | tf_op jit(solution)/shard_map/ppermute | solution.py:219
  35.3 2.7 %collective-permute-start.5 = (f32[128,512]{1,0:T(8,128)S(1)}, f32[128,512]{1,0:T(8,128)S(1)}, u32[]{:S(2)}, u32[]{:S(2)}) collective-permute-start(f32[128,512]{1,0:T(8,128)S(1)} %collective-permute-done.4.refs_2_), channel_id=1, source_target_pairs={{0,224},{32,0},{64,32},{96,64},{128,96},{160,128},{192,160},{224,1... | collective-permute-start | bytes 786440 | tf_op jit(solution)/shard_map/ppermute | solution.py:219
  41.1 3.8 %collective-permute-done.6.refs_3_ = f32[128,512]{1,0:T(8,128)S(1)} collective-permute-done((f32[128,512]{1,0:T(8,128)S(1)}, f32[128,512]{1,0:T(8,128)S(1)}, u32[]{:S(2)}, u32[]{:S(2)}) %collective-permute-start.6) | collective-permute-done | bytes 262176 | tf_op jit(solution)/shard_map/ppermute | solution.py:219
  48.1 6.3 %all-to-all-start.1 = ((f32[32,8,128]{2,1,0:T(8,128)}), f32[32,8,128]{2,1,0:T(8,128)S(1)}, u32[]{:S(2)}, u32[]{:S(2)}) async-start(f32[32,8,128]{2,1,0:T(8,128)} %bitcast.8), calls=%async_computation.1 | async-start | bytes 262144 | tf_op jit(solution)/shard_map/all_to_all | solution.py:233
  54.9 7.0 %collective-permute-done.2.refs_5_ = f32[128,512]{1,0:T(8,128)S(1)} collective-permute-done((f32[128,512]{1,0:T(8,128)S(1)}, f32[128,512]{1,0:T(8,128)S(1)}, u32[]{:S(2)}, u32[]{:S(2)}) %collective-permute-start.2) | collective-permute-done | bytes 262176 | tf_op jit(solution)/shard_map/ppermute | solution.py:219
  61.8 3.1 %all-to-all-done.1 = f32[32,8,128]{2,1,0:T(8,128)S(1)} async-done(((f32[32,8,128]{2,1,0:T(8,128)}), f32[32,8,128]{2,1,0:T(8,128)S(1)}, u32[]{:S(2)}, u32[]{:S(2)}) %all-to-all-start.1) | async-done | bytes 131104 | tf_op jit(solution)/shard_map/all_to_all | solution.py:233
  67.4 1.8 %shard_map.47 = (bf16[8,256,512]{2,1,0:T(8,128)(2,1)S(1)}, bf16[8,256,512]{2,1,0:T(8,128)(2,1)S(1)}) custom-call(s32[5]{0:T(128)S(1)} %stack.27.flags_ref, f32[128,512]{1,0:T(8,128)S(1)} %fusion.refs_0_, f32[128,512]{1,0:T(8,128)S(1)} %collective-permute-done.1.refs_1_, f32[128,512]{1,0:T(8,128)S(1)} %collective-permute-done.4.refs_2_, ...), custom_call_target="tpu_custom_call" | custom-call | tf_op jit(solution)/shard_map/pallas_call | solution.py:115
  70.5 2.3 %collective-permute-start.16 = (f32[13,8,256]{2,1,0:T(8,128)S(1)}, f32[13,8,256]{2,1,0:T(8,128)S(1)}, u32[]{:S(2)}, u32[]{:S(2)}) collective-permute-start(f32[13,8,256]{2,1,0:T(8,128)S(1)} %get-tuple-element.39), channel_id=1, source_target_pairs={{0,6},{1,7},{2,4},{3,5},{4,2},{5,3},{6,0},{7,1},{8,14},{9,15},{10,... | collective-permute-start | bytes 319496 | tf_op jit(solution)/shard_map/ppermute | solution.py:255
  73.6 4.4 %collective-permute-done.17.far_ref = f32[8,256]{1,0:T(8,128)S(1)} collective-permute-done((f32[8,256]{1,0:T(8,128)S(1)}, f32[8,256]{1,0:T(8,128)S(1)}, u32[]{:S(2)}, u32[]{:S(2)}) %collective-permute-start.17) | collective-permute-done | bytes 8224 | tf_op jit(solution)/shard_map/ppermute | solution.py:254
  80.9 3.3 %collective-permute-done.19.far_ref = f32[8,256]{1,0:T(8,128)S(1)} collective-permute-done((f32[8,256]{1,0:T(8,128)S(1)}, f32[8,256]{1,0:T(8,128)S(1)}, u32[]{:S(2)}, u32[]{:S(2)}) %collective-permute-start.19) | collective-permute-done | bytes 8224 | tf_op jit(solution)/shard_map/ppermute | solution.py:254
  86.5 1.8 %collective-permute-start.21 = (f32[8,256]{1,0:T(8,128)S(1)}, f32[8,256]{1,0:T(8,128)S(1)}, u32[]{:S(2)}, u32[]{:S(2)}) collective-permute-start(f32[8,256]{1,0:T(8,128)S(1)} %get-tuple-element.45), channel_id=1, source_target_pairs={{0,4},{1,5},{2,6},{3,7},{4,0},{5,1},{6,2},{7,3},{8,12},{9,13},{10,... | collective-permute-start | bytes 24584 | tf_op jit(solution)/shard_map/ppermute | solution.py:254
  88.3 3.4 %collective-permute-done.21.far_ref = f32[8,256]{1,0:T(8,128)S(1)} collective-permute-done((f32[8,256]{1,0:T(8,128)S(1)}, f32[8,256]{1,0:T(8,128)S(1)}, u32[]{:S(2)}, u32[]{:S(2)}) %collective-permute-start.21) | collective-permute-done | bytes 8224 | tf_op jit(solution)/shard_map/ppermute | solution.py:254
  92.5 2.2 %collective-permute-start.22 = (f32[7,8,256]{2,1,0:T(8,128)S(1)}, f32[7,8,256]{2,1,0:T(8,128)S(1)}, u32[]{:S(2)}, u32[]{:S(2)}) collective-permute-start(f32[7,8,256]{2,1,0:T(8,128)S(1)} %get-tuple-element.47), channel_id=1, source_target_pairs={{0,24},{1,25},{2,26},{3,27},{4,28},{5,29},{6,30},{7,31},{8,16},{9,... | collective-permute-start | bytes 172040 | tf_op jit(solution)/shard_map/ppermute | solution.py:255
  94.7 4.5 %collective-permute-done.23.far_ref = f32[8,256]{1,0:T(8,128)S(1)} collective-permute-done((f32[8,256]{1,0:T(8,128)S(1)}, f32[8,256]{1,0:T(8,128)S(1)}, u32[]{:S(2)}, u32[]{:S(2)}) %collective-permute-start.23) | collective-permute-done | bytes 8224 | tf_op jit(solution)/shard_map/ppermute | solution.py:254
  100.1 2.1 %collective-permute-start.24 = (f32[5,8,256]{2,1,0:T(8,128)S(1)}, f32[5,8,256]{2,1,0:T(8,128)S(1)}, u32[]{:S(2)}, u32[]{:S(2)}) collective-permute-start(f32[5,8,256]{2,1,0:T(8,128)S(1)} %get-tuple-element.50), channel_id=1, source_target_pairs={{0,6},{1,7},{2,4},{3,5},{4,2},{5,3},{6,0},{7,1},{8,14},{9,15},{10,... | collective-permute-start | bytes 122888 | tf_op jit(solution)/shard_map/ppermute | solution.py:255
  102.2 5.2 %collective-permute-done.25.far_ref = f32[8,256]{1,0:T(8,128)S(1)} collective-permute-done((f32[8,256]{1,0:T(8,128)S(1)}, f32[8,256]{1,0:T(8,128)S(1)}, u32[]{:S(2)}, u32[]{:S(2)}) %collective-permute-start.25) | collective-permute-done | bytes 8224 | tf_op jit(solution)/shard_map/ppermute | solution.py:254
  108.1 2.7 %collective-permute-start.27 = (f32[3,8,256]{2,1,0:T(8,128)S(1)}, f32[3,8,256]{2,1,0:T(8,128)S(1)}, u32[]{:S(2)}, u32[]{:S(2)}) collective-permute-start(f32[3,8,256]{2,1,0:T(8,128)S(1)} %get-tuple-element.54), channel_id=1, source_target_pairs={{0,8},{1,9},{2,10},{3,11},{4,12},{5,13},{6,14},{7,15},{8,0},{9,1},... | collective-permute-start | bytes 73736 | tf_op jit(solution)/shard_map/ppermute | solution.py:255
  110.8 4.5 %collective-permute-done.28.far_ref = f32[8,256]{1,0:T(8,128)S(1)} collective-permute-done((f32[8,256]{1,0:T(8,128)S(1)}, f32[8,256]{1,0:T(8,128)S(1)}, u32[]{:S(2)}, u32[]{:S(2)}) %collective-permute-start.28) | collective-permute-done | bytes 8224 | tf_op jit(solution)/shard_map/ppermute | solution.py:254
  118.3 2.6 %collective-permute-done.29.near_ref = f32[1,8,256]{2,1,0:T(8,128)S(1)} collective-permute-done((f32[1,8,256]{2,1,0:T(8,128)S(1)}, f32[1,8,256]{2,1,0:T(8,128)S(1)}, u32[]{:S(2)}, u32[]{:S(2)}) %collective-permute-start.29) | collective-permute-done | bytes 8224 | tf_op jit(solution)/shard_map/ppermute | solution.py:255
  123.1 11.6 %all_to_all.15 = f32[8,8,128]{2,1,0:T(8,128)S(1)} all-to-all(f32[8,8,128]{2,1,0:T(8,128)S(1)} %broadcast_in_dim.15), channel_id=1, replica_groups=mesh['row'=8,'quad'=8,'i'=4] {'row'}, dimensions={0} | all-to-all | bytes 65536 | tf_op jit(solution)/shard_map/all_to_all | solution.py:266
  (69 shorter events, 28.0 us)
Async XLA Ops:
  0.0 15.8 %collective-permute-start = (f32[512,128]{1,0:T(8,128)}, f32[512,128]{1,0:T(8,128)S(1)}, u32[]{:S(2)}, u32[]{:S(2)}) collective-permute-start(f32[512,128]{1,0:T(8,128)} %bitcast.19), channel_id=1, source_target_pairs={{0,6},{1,7},{2,4},{3,5},{4,2},{5,3},{6,0},{7,1},{16,22},{17,23},{1... | collective-permute-start | bytes 786440 | tf_op jit(solution)/shard_map/ppermute | solution.py:209
  6.4 39.8 %all-to-all-start = ((f32[32,64,128]{2,1,0:T(8,128)}), f32[32,64,128]{2,1,0:T(8,128)}, u32[]{:S(2)}, u32[]{:S(2)}) async-start(f32[32,64,128]{2,1,0:T(8,128)} %shard_map.46), calls=%async_computation | async-start | bytes 2097152 | tf_op jit(solution)/shard_map/all_to_all | solution.py:224
  17.1 18.3 %collective-permute-start.4 = (f32[128,512]{1,0:T(8,128)S(1)}, f32[128,512]{1,0:T(8,128)S(1)}, u32[]{:S(2)}, u32[]{:S(2)}) collective-permute-start(f32[128,512]{1,0:T(8,128)S(1)} %fusion.refs_0_), channel_id=1, source_target_pairs={{0,192},{32,224},{64,0},{96,32},{128,64},{160,96},{192,128},{224,1... | collective-permute-start | bytes 786440 | tf_op jit(solution)/shard_map/ppermute | solution.py:219
  23.4 16.1 %collective-permute-start.1 = (f32[128,512]{1,0:T(8,128)S(1)}, f32[128,512]{1,0:T(8,128)S(1)}, u32[]{:S(2)}, u32[]{:S(2)}) collective-permute-start(f32[128,512]{1,0:T(8,128)S(1)} %fusion.refs_0_), channel_id=1, source_target_pairs={{0,64},{32,96},{64,128},{96,160},{128,192},{160,224},{192,0},{224,... | collective-permute-start | bytes 786440 | tf_op jit(solution)/shard_map/ppermute | solution.py:219
  23.4 17.6 %collective-permute-start.7 = (f32[128,512]{1,0:T(8,128)S(1)}, f32[128,512]{1,0:T(8,128)S(1)}, u32[]{:S(2)}, u32[]{:S(2)}) collective-permute-start(f32[128,512]{1,0:T(8,128)S(1)} %fusion.refs_0_), channel_id=1, source_target_pairs={{0,224},{32,0},{64,32},{96,64},{128,96},{160,128},{192,160},{224,1... | collective-permute-start | bytes 786440 | tf_op jit(solution)/shard_map/ppermute | solution.py:219
  27.1 17.8 %collective-permute-start.6 = (f32[128,512]{1,0:T(8,128)S(1)}, f32[128,512]{1,0:T(8,128)S(1)}, u32[]{:S(2)}, u32[]{:S(2)}) collective-permute-start(f32[128,512]{1,0:T(8,128)S(1)} %fusion.refs_0_), channel_id=1, source_target_pairs={{0,32},{32,64},{64,96},{96,128},{128,160},{160,192},{192,224},{224... | collective-permute-start | bytes 786440 | tf_op jit(solution)/shard_map/ppermute | solution.py:219
  35.3 10.8 %collective-permute-start.5 = (f32[128,512]{1,0:T(8,128)S(1)}, f32[128,512]{1,0:T(8,128)S(1)}, u32[]{:S(2)}, u32[]{:S(2)}) collective-permute-start(f32[128,512]{1,0:T(8,128)S(1)} %collective-permute-done.4.refs_2_), channel_id=1, source_target_pairs={{0,224},{32,0},{64,32},{96,64},{128,96},{160,128},{192,160},{224,1... | collective-permute-start | bytes 786440 | tf_op jit(solution)/shard_map/ppermute | solution.py:219
  39.5 14.9 %collective-permute-start.3 = (f32[128,512]{1,0:T(8,128)S(1)}, f32[128,512]{1,0:T(8,128)S(1)}, u32[]{:S(2)}, u32[]{:S(2)}) collective-permute-start(f32[128,512]{1,0:T(8,128)S(1)} %collective-permute-done.1.refs_1_), channel_id=1, source_target_pairs={{0,32},{32,64},{64,96},{96,128},{128,160},{160,192},{192,224},{224... | collective-permute-start | bytes 786440 | tf_op jit(solution)/shard_map/ppermute | solution.py:219
  40.5 21.3 %collective-permute-start.2 = (f32[128,512]{1,0:T(8,128)S(1)}, f32[128,512]{1,0:T(8,128)S(1)}, u32[]{:S(2)}, u32[]{:S(2)}) collective-permute-start(f32[128,512]{1,0:T(8,128)S(1)} %collective-permute-done.1.refs_1_), channel_id=1, source_target_pairs={{0,64},{32,96},{64,128},{96,160},{128,192},{160,224},{192,0},{224,... | collective-permute-start | bytes 786440 | tf_op jit(solution)/shard_map/ppermute | solution.py:219
  41.1 23.9 %collective-permute-start.8 = (f32[128,512]{1,0:T(8,128)S(1)}, f32[128,512]{1,0:T(8,128)S(1)}, u32[]{:S(2)}, u32[]{:S(2)}) collective-permute-start(f32[128,512]{1,0:T(8,128)S(1)} %fusion.refs_0_), channel_id=1, source_target_pairs={{0,1},{1,0},{2,3},{3,2},{4,5},{5,4},{6,7},{7,6},{8,9},{9,8},{10,11... | collective-permute-start | bytes 786440 | tf_op jit(solution)/shard_map/ppermute | solution.py:229
  44.9 20.1 %collective-permute-start.12 = (f32[128,512]{1,0:T(8,128)S(1)}, f32[128,512]{1,0:T(8,128)S(1)}, u32[]{:S(2)}, u32[]{:S(2)}) collective-permute-start(f32[128,512]{1,0:T(8,128)S(1)} %collective-permute-done.7.refs_4_), channel_id=1, source_target_pairs={{0,1},{1,0},{2,3},{3,2},{4,5},{5,4},{6,7},{7,6},{8,9},{9,8},{10,11... | collective-permute-start | bytes 786440 | tf_op jit(solution)/shard_map/ppermute | solution.py:229
  46.2 19.3 %collective-permute-start.11 = (f32[128,512]{1,0:T(8,128)S(1)}, f32[128,512]{1,0:T(8,128)S(1)}, u32[]{:S(2)}, u32[]{:S(2)}) collective-permute-start(f32[128,512]{1,0:T(8,128)S(1)} %collective-permute-done.6.refs_3_), channel_id=1, source_target_pairs={{0,1},{1,0},{2,3},{3,2},{4,5},{5,4},{6,7},{7,6},{8,9},{9,8},{10,11... | collective-permute-start | bytes 786440 | tf_op jit(solution)/shard_map/ppermute | solution.py:229
  48.1 16.8 %all-to-all-start.1 = ((f32[32,8,128]{2,1,0:T(8,128)}), f32[32,8,128]{2,1,0:T(8,128)S(1)}, u32[]{:S(2)}, u32[]{:S(2)}) async-start(f32[32,8,128]{2,1,0:T(8,128)} %bitcast.8), calls=%async_computation.1 | async-start | bytes 262144 | tf_op jit(solution)/shard_map/all_to_all | solution.py:233
  54.5 11.4 %collective-permute-start.10 = (f32[128,512]{1,0:T(8,128)S(1)}, f32[128,512]{1,0:T(8,128)S(1)}, u32[]{:S(2)}, u32[]{:S(2)}) collective-permute-start(f32[128,512]{1,0:T(8,128)S(1)} %collective-permute-done.4.refs_2_), channel_id=1, source_target_pairs={{0,1},{1,0},{2,3},{3,2},{4,5},{5,4},{6,7},{7,6},{8,9},{9,8},{10,11... | collective-permute-start | bytes 786440 | tf_op jit(solution)/shard_map/ppermute | solution.py:229
  70.5 7.5 %collective-permute-start.16 = (f32[13,8,256]{2,1,0:T(8,128)S(1)}, f32[13,8,256]{2,1,0:T(8,128)S(1)}, u32[]{:S(2)}, u32[]{:S(2)}) collective-permute-start(f32[13,8,256]{2,1,0:T(8,128)S(1)} %get-tuple-element.39), channel_id=1, source_target_pairs={{0,6},{1,7},{2,4},{3,5},{4,2},{5,3},{6,0},{7,1},{8,14},{9,15},{10,... | collective-permute-start | bytes 319496 | tf_op jit(solution)/shard_map/ppermute | solution.py:255
  72.8 5.2 %collective-permute-start.17 = (f32[8,256]{1,0:T(8,128)S(1)}, f32[8,256]{1,0:T(8,128)S(1)}, u32[]{:S(2)}, u32[]{:S(2)}) collective-permute-start(f32[8,256]{1,0:T(8,128)S(1)} %get-tuple-element.40), channel_id=1, source_target_pairs={{0,4},{1,5},{2,6},{3,7},{4,0},{5,1},{6,2},{7,3},{8,12},{9,13},{10,... | collective-permute-start | bytes 24584 | tf_op jit(solution)/shard_map/ppermute | solution.py:254
  79.0 5.2 %collective-permute-start.18 = (f32[11,8,256]{2,1,0:T(8,128)S(1)}, f32[11,8,256]{2,1,0:T(8,128)S(1)}, u32[]{:S(2)}, u32[]{:S(2)}) collective-permute-start(f32[11,8,256]{2,1,0:T(8,128)S(1)} %get-tuple-element.41), channel_id=1, source_target_pairs={{0,8},{1,9},{2,10},{3,11},{4,12},{5,13},{6,14},{7,15},{8,0},{9,1},... | collective-permute-start | bytes 270344 | tf_op jit(solution)/shard_map/ppermute | solution.py:255
  85.2 6.5 %collective-permute-start.20 = (f32[9,8,256]{2,1,0:T(8,128)S(1)}, f32[9,8,256]{2,1,0:T(8,128)S(1)}, u32[]{:S(2)}, u32[]{:S(2)}) collective-permute-start(f32[9,8,256]{2,1,0:T(8,128)S(1)} %get-tuple-element.44), channel_id=1, source_target_pairs={{0,6},{1,7},{2,4},{3,5},{4,2},{5,3},{6,0},{7,1},{8,14},{9,15},{10,... | collective-permute-start | bytes 221192 | tf_op jit(solution)/shard_map/ppermute | solution.py:255
  86.5 5.2 %collective-permute-start.21 = (f32[8,256]{1,0:T(8,128)S(1)}, f32[8,256]{1,0:T(8,128)S(1)}, u32[]{:S(2)}, u32[]{:S(2)}) collective-permute-start(f32[8,256]{1,0:T(8,128)S(1)} %get-tuple-element.45), channel_id=1, source_target_pairs={{0,4},{1,5},{2,6},{3,7},{4,0},{5,1},{6,2},{7,3},{8,12},{9,13},{10,... | collective-permute-start | bytes 24584 | tf_op jit(solution)/shard_map/ppermute | solution.py:254
  92.5 6.8 %collective-permute-start.22 = (f32[7,8,256]{2,1,0:T(8,128)S(1)}, f32[7,8,256]{2,1,0:T(8,128)S(1)}, u32[]{:S(2)}, u32[]{:S(2)}) collective-permute-start(f32[7,8,256]{2,1,0:T(8,128)S(1)} %get-tuple-element.47), channel_id=1, source_target_pairs={{0,24},{1,25},{2,26},{3,27},{4,28},{5,29},{6,30},{7,31},{8,16},{9,... | collective-permute-start | bytes 172040 | tf_op jit(solution)/shard_map/ppermute | solution.py:255
  100.1 7.2 %collective-permute-start.24 = (f32[5,8,256]{2,1,0:T(8,128)S(1)}, f32[5,8,256]{2,1,0:T(8,128)S(1)}, u32[]{:S(2)}, u32[]{:S(2)}) collective-permute-start(f32[5,8,256]{2,1,0:T(8,128)S(1)} %get-tuple-element.50), channel_id=1, source_target_pairs={{0,6},{1,7},{2,4},{3,5},{4,2},{5,3},{6,0},{7,1},{8,14},{9,15},{10,... | collective-permute-start | bytes 122888 | tf_op jit(solution)/shard_map/ppermute | solution.py:255
  102.2 5.2 %collective-permute-start.25 = (f32[8,256]{1,0:T(8,128)S(1)}, f32[8,256]{1,0:T(8,128)S(1)}, u32[]{:S(2)}, u32[]{:S(2)}) collective-permute-start(f32[8,256]{1,0:T(8,128)S(1)} %get-tuple-element.51), channel_id=1, source_target_pairs={{0,4},{1,5},{2,6},{3,7},{4,0},{5,1},{6,2},{7,3},{8,12},{9,13},{10,... | collective-permute-start | bytes 24584 | tf_op jit(solution)/shard_map/ppermute | solution.py:254
  108.1 7.3 %collective-permute-start.27 = (f32[3,8,256]{2,1,0:T(8,128)S(1)}, f32[3,8,256]{2,1,0:T(8,128)S(1)}, u32[]{:S(2)}, u32[]{:S(2)}) collective-permute-start(f32[3,8,256]{2,1,0:T(8,128)S(1)} %get-tuple-element.54), channel_id=1, source_target_pairs={{0,8},{1,9},{2,10},{3,11},{4,12},{5,13},{6,14},{7,15},{8,0},{9,1},... | collective-permute-start | bytes 73736 | tf_op jit(solution)/shard_map/ppermute | solution.py:255
  117.7 5.4 %collective-permute-start.26 = (f32[8,256]{1,0:T(8,128)S(1)}, f32[8,256]{1,0:T(8,128)S(1)}, u32[]{:S(2)}, u32[]{:S(2)}) collective-permute-start(f32[8,256]{1,0:T(8,128)S(1)} %get-tuple-element.53.final_ref), channel_id=1, source_target_pairs={{0,6},{1,7},{2,4},{3,5},{4,2},{5,3},{6,0},{7,1},{16,22},{17,23},{1... | collective-permute-start | bytes 24584 | tf_op jit(solution)/shard_map/ppermute | solution.py:209
  (13 other events, 61.9 us)
